TPU v7x, 256 devices: a whole 4x4x8 slice. The times are simulated.
256 devices in a mesh: ga: 32 (over y, x, z_hi), band: 8 (over z_lo, core).
Axes of the slice: x: 4, y: 4, z: 8 (z_hi: 2, z_lo: 4; z = z_hi * 4 + z_lo), core: 2. Of those that a mesh axis runs over, the one named last changes fastest.
Arguments:
- coefficients: float32 [2048, 2, 16384], P('band', None, 'ga'), may hold values from -6 to 6
- rotation: float32 [2, 2048, 256], P(None, 'band', 'ga'), may hold values from -0.1875 to 0.1875
- potential: float32 [64, 4096], P(None, 'ga'), may hold values from -2 to 0.5
- index_map: int32 [16384], replicated, may hold values from 0 to 262143, as said below
- counts: int32 [32], replicated, may hold values from 384 to 512, as said below
Outputs:
- applied_panel: float32 [256, 2, 32, 1024], P(('band', 'ga'))
Inputs may be any that keep to these rules, and one draw needn't show every extreme that they name: counts[i] counts the live slots of index i of ga, which are its slots 0 to counts[i] - 1 of 512; the counts sum to 14336, and some index has exactly 512. `index_map`: live slots name distinct cells, and together exactly 14336 cells whose signed frequency vector has a squared length no larger than that of any cell not named (a ball about the anchor), every signed component of a live cell lying in -16 to 15; dead slots name arbitrary cells.
All inputs are finite; a program needn't handle non-finite values.
Results may differ from a plain program's by a relative error of at most 0.00008.
Values sent between devices are 32-bit elements; how exact they have to be, the bound alone decides.
A program may use at most 128 MiB of HBM per device.

v0:
```python
import math

import jax
import jax.numpy as jnp
from jax import lax
from jax.sharding import Mesh
from jax.sharding import PartitionSpec as P

GA = ("ga_0", "ga_1", "ga_2")
BAND = ("band_0", "band_1")
BAND_GA = ("band_0", "band_1", "ga_0", "ga_1", "ga_2")


def in_order(parts, dim):
    parts = jnp.moveaxis(parts, 0, dim)
    dims = parts.shape
    return parts.reshape(*dims[:dim], dims[dim] * dims[dim + 1], *dims[dim + 2 :])


def gather_in_order(value, axes, order):
    parts = value
    for k in order:
        parts = lax.all_gather(parts, axes[k])
    done = order[::-1]
    back = [done.index(k) for k in range(len(axes))]
    parts = parts.transpose(*back, *range(len(axes), parts.ndim))
    return parts.reshape(-1, *value.shape)


def gather_axes(value, axes, order, dim):
    return in_order(gather_in_order(value, axes, order), dim)


def cut_along(value, dim, peers):
    dims = value.shape
    parts = value.reshape(*dims[:dim], peers, dims[dim] // peers, *dims[dim + 1 :])
    return jnp.moveaxis(parts, dim, 0)


def sum_by_chip(value, chips, core, dim):
    sizes = (lax.axis_size(chips), lax.axis_size(core))
    parts = cut_along(value, dim, sizes[0] * sizes[1])
    inside = parts.shape[1:]
    parts = parts.reshape(*sizes, *inside).swapaxes(0, 1).reshape(-1, *inside)
    parts = lax.psum_scatter(parts, core, scatter_dimension=0, tiled=True)
    return lax.psum_scatter(parts, chips, scatter_dimension=0, tiled=True)[0]


def items_in_groups(value, axis, split_dim, concat_dim, work, item_dim, out_dim):
    items = jax.tree.leaves(value)[0].shape[item_dim]
    count = 2 if items % 2 == 0 else 1
    done = []
    for k in range(count):
        group = jax.tree.map(
            lambda a: lax.slice_in_dim(
                a, k * (items // count), (k + 1) * (items // count), axis=item_dim
            ),
            value,
        )
        done.append(
            work(
                lax.all_to_all(
                    group, axis, split_axis=split_dim, concat_axis=concat_dim, tiled=True
                )
            )
        )
    return jax.tree.map(lambda *parts: jnp.concatenate(parts, axis=out_dim), *done)


def mixing(columns):
    real_cols = columns[0].T
    imag_cols = columns[1].T
    upper_rows = jnp.stack([real_cols, -imag_cols], axis=-1)
    lower_rows = jnp.stack([imag_cols, real_cols], axis=-1)
    stacked = jnp.stack([upper_rows, lower_rows], axis=1)
    return stacked.reshape(2 * real_cols.shape[0], 2 * real_cols.shape[1])


def window_kinetic(box_edge, window):
    signed = (jnp.arange(window, dtype=jnp.int32) - window // 2).astype(jnp.float32)
    squared = signed[:, None, None] ** 2 + signed[None, :, None] ** 2 + signed[None, None, :] ** 2
    return 8.0 / (box_edge * box_edge) * squared


def dft_tables(box_edge, window):
    signed = jnp.arange(window, dtype=jnp.int32) - window // 2
    ticks_index = jnp.arange(box_edge, dtype=jnp.int32)
    inv_phase = ticks_index[:, None] * signed[None, :] % box_edge
    inv_angles = inv_phase.astype(jnp.float32) * (2.0 * math.pi / box_edge)
    inv_cos = jnp.cos(inv_angles)
    inv_sin = jnp.sin(inv_angles)
    inverse = (
        jnp.stack([jnp.stack([inv_cos, -inv_sin], 1), jnp.stack([inv_sin, inv_cos], 1)], 0)
        / box_edge
    )
    fwd_phase = signed[:, None] * ticks_index[None, :] % box_edge
    fwd_angles = fwd_phase.astype(jnp.float32) * (2.0 * math.pi / box_edge)
    fwd_cos = jnp.cos(fwd_angles)
    fwd_sin = jnp.sin(fwd_angles)
    forward = jnp.stack([jnp.stack([fwd_cos, fwd_sin], 1), jnp.stack([-fwd_sin, fwd_cos], 1)], 0)
    return (forward, inverse)


def transform(grid_field, dft_table):
    grid_field = jnp.einsum(
        "dkcn,cnyz->dkyz", dft_table, grid_field, precision=lax.Precision.HIGHEST
    )
    grid_field = jnp.einsum(
        "dkcn,cxnz->dxkz", dft_table, grid_field, precision=lax.Precision.HIGHEST
    )
    return jnp.einsum("dkcn,cxyn->dxyk", dft_table, grid_field, precision=lax.Precision.HIGHEST)


def per_device(coefficients, rotation, potential, index_map, counts):
    rot_full, pot_full = (
        gather_axes(rotation, GA, (2, 0, 1), 2),
        gather_axes(potential, GA, (2, 0, 1), 1),
    )
    band_local = coefficients.shape[0]
    slot_local = coefficients.shape[2]
    flat_coeffs = coefficients.reshape(2 * band_local, slot_local)
    box_edge = pot_full.shape[0]
    window = box_edge // 2
    half_window = window // 2
    window_cells = window * window * window
    slots_each = index_map.shape[0] // counts.shape[0]
    slot_ids = jnp.arange(slots_each, dtype=jnp.int32)
    live_mask = (slot_ids[None, :] < counts[:, None]).reshape(-1).astype(jnp.float32)
    cell_x = (index_map // (box_edge * box_edge) + half_window) % box_edge
    cell_y = (index_map // box_edge % box_edge + half_window) % box_edge
    cell_z = (index_map % box_edge + half_window) % box_edge
    inside = (cell_x < window) & (cell_y < window) & (cell_z < window)
    window_index = jnp.where(inside, (cell_x * window + cell_y) * window + cell_z, window_cells)
    kinetic = window_kinetic(box_edge, window)
    pot_grid = pot_full.reshape(box_edge, box_edge, box_edge)
    forward, inverse = dft_tables(box_edge, window)

    def apply_one(values):
        masked = values * live_mask[None, :]
        box_cells = (
            jnp.zeros((2, window_cells), jnp.float32).at[:, window_index].add(masked, mode="drop")
        )
        grid_field = box_cells.reshape(2, window, window, window)
        real_space = transform(grid_field, inverse)
        applied = transform(pot_grid[None] * real_space, forward) + kinetic[None] * grid_field
        return applied.reshape(2, window, window * window)

    def apply_bands(received):
        return lax.map(apply_one, received[0])

    panel_rows = rot_full.shape[2] // lax.axis_size(BAND)
    product = jnp.dot(mixing(rot_full), flat_coeffs, precision=lax.Precision.HIGHEST)
    summed = sum_by_chip(
        product.reshape(
            panel_rows * lax.axis_size("band_0") * lax.axis_size("band_1"), 2, slot_local
        ),
        "band_0",
        "band_1",
        0,
    )
    groups = lax.axis_size(GA)
    grouped = summed.reshape(groups, panel_rows // groups, 2, slot_local)
    return items_in_groups(grouped, GA, 0, 3, apply_bands, 1, 0)


def solution(mesh):
    torus = Mesh(mesh.devices.reshape(4, 4, 2, 4, 2), ("ga_0", "ga_1", "ga_2", "band_0", "band_1"))
    placed = (P(BAND, None, GA), P(None, BAND, GA), P(None, GA), P(), P())
    return jax.shard_map(
        per_device,
        mesh=torus,
        in_specs=placed,
        out_specs=P(BAND_GA, None, None, None),
        check_vma=False,
    )
```

profile of v0, /device:TPU:32, one launch (start us, length us, event | category | flops | bytes accessed | tf_op | source)
XLA Modules:
  0.0 273.7 jit_solution(14999911714070826652)
XLA Ops:
  7.4 8.9 %all-gather.3 = f32[4,256,8]{1,2,0:T(8,128)S(1)} all-gather(f32[2,256,8]{1,2,0:T(8,128)} %param.6), channel_id=5, replica_groups=mesh['ga_0'=4,'ga_1'=4,'ga_2'=2,'band_0'=4,'band_1'=2] {'ga_2'}, dimensions={0}, use_global_device_ids=true | all-gather | bytes 49152 | tf_op jit(solution)/shard_map/all_gather | solution.py:23
  16.3 12.5 %all-gather.4 = f32[8,2,256,8]{2,3,1,0:T(8,128)S(1)} all-gather(f32[2,2,256,8]{2,3,1,0:T(8,128)S(1)} %bitcast.151), channel_id=6, replica_groups=mesh['ga_0'=4,'ga_1'=4,'ga_2'=2,'band_0'=4,'band_1'=2] {'ga_0'}, dimensions={0}, use_global_device_ids=true | all-gather | bytes 163840 | tf_op jit(solution)/shard_map/all_gather | solution.py:23
  28.8 13.8 %all-gather.5 = f32[16,2,2,256,8]{3,4,2,1,0:T(8,128)S(1)} all-gather(f32[4,2,2,256,8]{3,4,2,1,0:T(8,128)S(1)} %bitcast.147), channel_id=7, replica_groups=mesh['ga_0'=4,'ga_1'=4,'ga_2'=2,'band_0'=4,'band_1'=2] {'ga_1'}, dimensions={0}, use_global_device_ids=true | all-gather | bytes 655360 | tf_op jit(solution)/shard_map/all_gather | solution.py:23
  43.0 1.9 stack.76
  45.0 2.4 copy.71
  47.6 1.9 stack.79
  51.0 1.9 reshape.369
  53.0 1.8 convolution_bitcast_fusion.2
  56.0 14.7 %reduce-scatter.3.cloned.1.call-done = f32[4,32,2,512]{3,1,2,0:T(8,128)} async-done(((f32[8,32,2,512]{3,1,2,0:T(8,128)}), f32[4,32,2,512]{3,1,2,0:T(8,128)}) %reduce-scatter.3.cloned.1.call-update) | async-done | bytes 524304 | tf_op jit(solution)/shard_map/reduce_scatter | solution.py:45
  70.7 8.5 %all-gather = f32[128,128]{1,0:T(8,128)S(1)} all-gather(f32[64,128]{1,0:T(8,128)S(1)} %copy-done.4), channel_id=2, replica_groups=mesh['ga_0'=4,'ga_1'=4,'ga_2'=2,'band_0'=4,'band_1'=2] {'ga_2'}, dimensions={0}, use_global_device_ids=true | all-gather | bytes 98304 | tf_op jit(solution)/shard_map/all_gather | solution.py:23
  79.2 13.3 %all-gather.1 = f32[8,64,128]{2,1,0:T(8,128)} all-gather(f32[2,64,128]{2,1,0:T(8,128)S(1)} %bitcast.150), channel_id=3, replica_groups=mesh['ga_0'=4,'ga_1'=4,'ga_2'=2,'band_0'=4,'band_1'=2] {'ga_0'}, dimensions={0}, use_global_device_ids=true | all-gather | bytes 327680 | tf_op jit(solution)/shard_map/all_gather | solution.py:23
  93.3 5.0 %reduce-scatter.5.cloned.1.call-done = f32[1,32,2,512]{3,1,2,0:T(8,128)} async-done(((f32[4,32,2,512]{3,1,2,0:T(8,128)}), f32[1,32,2,512]{3,1,2,0:T(8,128)}) %reduce-scatter.5.cloned.1.call-update) | async-done | bytes 131088 | tf_op jit(solution)/shard_map/reduce_scatter | solution.py:46
  100.0 12.7 %all-to-all-start = ((f32[32,1,2,512]{3,2,1,0:T(2,128)}), f32[32,1,2,512]{3,2,1,0:T(2,128)S(1)}, u32[]{:S(2)}, u32[]{:S(2)}) async-start(f32[32,1,2,512]{3,2,1,0:T(2,128)} %copy.74), calls=%async_computation.2 | async-start | bytes 262144 | tf_op jit(solution)/shard_map/all_to_all | solution.py:62
  113.7 7.1 %all-gather.8.cloned.1.call-done = f32[16,2,64,128]{3,2,1,0:T(8,128)} async-done(((f32[4,2,64,128]{3,2,1,0:T(8,128)}), f32[16,2,64,128]{3,2,1,0:T(8,128)}) %all-gather.8.cloned.1.call-update) | async-done | bytes 1048592 | tf_op jit(solution)/shard_map/all_gather | solution.py:23
  125.2 4.9 %copy.75 = f32[16384,2]{1,0:T(8,128)} copy(f32[16384,2]{0,1:T(2,128)S(1)} %multiply_bitcast_fusion) | data formatting | bytes 262144 | tf_op jit(solution)/shard_map/while/body/eval_jaxpr/mul | solution.py:139
  130.1 94.4 %scatter_custom_fusion = f32[2,32768]{0,1:T(8,128)} fusion(s32[16384]{0:T(1024)S(1)} %compare_select_fusion, f32[16384,2]{1,0:T(8,128)} %copy.75, f32[]{:T(128)} %constant.98.clone.1), kind=kCustom, calls=%fused_computation.1 | custom fusion | flops 32768 | bytes 262656 | tf_op jit(solution)/shard_map/while/body/eval_jaxpr/scatter-add | solution.py:141
  224.5 10.7 %copy.77 = f32[2,32,32,32]{1,3,0,2:T(8,128)S(1)} copy(f32[2,32,32,32]{0,3,2,1:T(8,128)} %bitcast.138) | data formatting | bytes 524288 | tf_op jit(solution)/shard_map/while/body/eval_jaxpr/reshape | solution.py:143
  235.2 10.5 %copy.81 = f32[2,32,32,32]{3,2,0,1:T(8,128)S(1)} copy(f32[2,32,32,32]{0,3,2,1:T(8,128)} %bitcast.139) | data formatting | bytes 524288 | tf_op jit(solution)/shard_map/while/body/eval_jaxpr/reshape | solution.py:143
  245.7 2.0 convolution_bitcast_fusion.1
  247.7 3.0 %copy.86 = f32[2,64,32,32,1]{2,3,0,4,1:T(8,128)S(1)} copy(f32[2,64,32,32,1]{1,3,2,0,4:T(8,128)} %convolution_bitcast_fusion.1) | data formatting | bytes 1048576 | tf_op jit(solution)/shard_map/while/body/eval_jaxpr/dkcn,cnyz->dkyz/dot_general | solution.py:105
  250.7 1.9 fusion.32
  252.6 3.6 %fusion.4 = f32[2,64,64,64]{3,2,0,1:T(8,128)S(1)} fusion(f32[64,32,2,64,1]{3,1,4,2,0:T(8,128)S(1)} %fusion.32, f32[64,64,64]{2,1,0:T(8,128)S(1)} %copy-done, f32[1,64,2,32]{1,3,2,0:T(8,128)S(1)} %get-tuple-element.38, f32[1,64,2,32]{1,3,2,0:T(8,128)S(1)} %get-tuple-element.36), kind=kOutput, calls=%fused_computation.6 | convolution fusion | flops 403193856 | bytes 4227072 | tf_op jit(solution)/shard_map/while/body/eval_jaxpr/dkcn,cxyn->dxyk/dot_general | solution.py:111
  256.3 5.1 %fusion.9 = f32[2,32,64,64,1]{3,1,2,0,4:T(8,128)S(1)} fusion(f32[2,64,64,64]{3,2,0,1:T(8,128)S(1)} %fusion.4, f32[1,32,2,64]{3,1,2,0:T(8,128)S(1)} %get-tuple-element.26, f32[1,32,2,64]{3,1,2,0:T(8,128)S(1)} %get-tuple-element.25), kind=kOutput, calls=%fused_computation.11 | convolution fusion | flops 402661376 | bytes 3178496 | tf_op jit(solution)/shard_map/while/body/eval_jaxpr/dkcn,cnyz->dkyz/dot_general | solution.py:105
  261.4 2.5 fusion.12
  (46 shorter events, 13.4 us)
Async XLA Ops:
  7.4 63.3 %reduce-scatter.3.cloned.1.call-start = ((), (), s32[]{:S(2)}) async-start(), calls=%async_computation.3 | async-start | bytes 1572864 | tf_op jit(solution)/shard_map/reduce_scatter | solution.py:45
  49.5 3.4 %copy-start.2 = (f32[4,2,32,1,512]{4,2,3,1,0:T(8,128)S(1)}, f32[4,2,32,1,512]{4,2,3,1,0:T(8,128)}, u32[]{:S(2)}) copy-start(f32[4,2,32,1,512]{4,2,3,1,0:T(8,128)} %copy.71) | copy-start | bytes 1572868
  54.8 15.9 %copy-start.4 = (f32[64,128]{1,0:T(8,128)S(1)}, f32[64,128]{1,0:T(8,128)}, u32[]{:S(2)}) copy-start(f32[64,128]{1,0:T(8,128)} %param.7) | copy-start | bytes 98308
  54.8 38.2 %copy-start.5 = (s32[32]{0:T(128)S(1)}, s32[32]{0:T(128)}, u32[]{:S(2)}) copy-start(s32[32]{0:T(128)} %param.9) | copy-start | bytes 388
  54.8 38.3 %copy-start.3 = (s32[16384]{0:T(1024)S(1)}, s32[16384]{0:T(1024)}, u32[]{:S(2)}) copy-start(s32[16384]{0:T(1024)} %param.8) | copy-start | bytes 196612
  56.0 42.4 %reduce-scatter.5.cloned.1.call-start = ((), (), s32[]{:S(2)}) async-start(), calls=%async_computation.4 | async-start | bytes 655360 | tf_op jit(solution)/shard_map/reduce_scatter | solution.py:46
  70.7 50.1 %all-gather.8.cloned.1.call-start = ((), (), s32[]{:S(2)}) async-start(), calls=%async_computation.5 | async-start | bytes 1310720 | tf_op jit(solution)/shard_map/all_gather | solution.py:23
  100.0 25.1 %all-to-all-start = ((f32[32,1,2,512]{3,2,1,0:T(2,128)}), f32[32,1,2,512]{3,2,1,0:T(2,128)S(1)}, u32[]{:S(2)}, u32[]{:S(2)}) async-start(f32[32,1,2,512]{3,2,1,0:T(2,128)} %copy.74), calls=%async_computation.2 | async-start | bytes 262144 | tf_op jit(solution)/shard_map/all_to_all | solution.py:62
  250.7 1.9 copy-start
  261.3 2.5 copy-start.1
Sparse Core Ops, SparseCore 0:
  56.1 14.5 reduce-scatter.2
  73.2 25.0 reduce-scatter.4
Sparse Core Ops, SparseCore 1:
  92.7 28.1 all-gather.7
where the time goes:
time: 274 us
  other arithmetic  96.3 us (35%)
  blocking collectives  57 us (21%)
  local copies, waits for them, and re-layouts  47.1 us (17%)
  waiting for transfers between devices  27.4 us (10%)
  matrix products  17.9 us (7%)
  between operations  15.2 us (6%)
  starting transfers between devices  12.7 us (5%)
    scatter-add x1, other arithmetic, apply_one(): jnp.zeros((2, window_cells), jnp.float32).at[:, window_index]  94.4 us
    all_gather x5, blocking collectives, gather_in_order(): parts = lax.all_gather(parts, axes[k])  57 us
    reshape x2, local copies, waits for them, and re-layouts, apply_one(): grid_field = box_cells.reshape(2, window, window, window)  21.2 us
    reduce_scatter x1, waiting for transfers between devices, sum_by_chip(): parts = lax.psum_scatter(parts, core, scatter_dimension=0, tiled=True)  14.7 us
    all_to_all x1, starting transfers between devices, items_in_groups(): lax.all_to_all(group, axis, split_axis=split_dim, concat_axis=concat_dim,...  12.7 us
    another operation x4, local copies, waits for them, and re-layouts, mixing(): stacked = jnp.stack([upper_rows, lower_rows], axis=1)  7.69 us
    all_gather x1, waiting for transfers between devices, gather_in_order(): parts = lax.all_gather(parts, axes[k])  7.13 us
    dot_general x2, matrix products, transform(): jnp.einsum('dkcn,cnyz->dkyz', dft_table, grid_field, precision=lax.Precis...  7.08 us
  transfers between devices with their start and end apart: 4, of which 4 were waited for; matrix products, arithmetic and copies ran while one was open for 3% of the time, Pallas kernels for 0%

commit v1 on v0

v1 whole, which is shorter than its diff:
```python
import math
import numpy as np
import jax
import jax.numpy as jnp
from jax import lax
from jax.experimental import pallas as pl
from jax.experimental.pallas import tpu as pltpu

F32 = jnp.float32
BF = jnp.bfloat16
HS = 72
FS = 40


def split_np(a):
    a = np.asarray(a, np.float32)
    hi = a.astype(BF)
    lo = (a - hi.astype(np.float32)).astype(BF)
    return hi, lo


def stack3(a):
    hi, lo = split_np(a)
    return np.concatenate([hi, hi, lo], axis=1)


def tables():
    n = np.arange(32) - 16
    r = np.arange(64)
    ang = 2.0 * math.pi * ((r[:, None] * n[None, :]) % 64) / 64.0
    cos, sin = np.cos(ang), np.sin(ang)
    perm = np.array([(k % 8) * 4 + k // 8 for k in range(32)])
    s = 8.0 / 4096.0
    wz = np.zeros((2, 4, 32, 2, 4, 2, 64))
    for q in range(4):
        wz[0, q, :, 0, q, 0, :] = cos.T / 64
        wz[1, q, :, 0, q, 0, :] = -sin.T / 64
        wz[0, q, :, 0, q, 1, :] = sin.T / 64
        wz[1, q, :, 0, q, 1, :] = cos.T / 64
    wz[:, :, :, 1] = wz[:, :, :, 0] * (s * n * n)[None, None, :, None, None, None]
    wz_h, wz_l = split_np(wz.reshape(256, 1024))
    ty = stack3(np.concatenate([cos[:, perm], sin[:, perm]], axis=1) / 64)
    tx = stack3(np.concatenate([cos, sin], axis=1) / 64)
    fx = stack3(np.concatenate([cos.T, sin.T], axis=0))
    fy = stack3(np.concatenate([cos.T[perm], sin.T[perm]], axis=0))
    wf = np.zeros((4, 2, 64, 2, 4, 32))
    for q in range(4):
        wf[q, 0, :, 0, q, :] = cos
        wf[q, 1, :, 0, q, :] = sin
        wf[q, 1, :, 1, q, :] = cos
        wf[q, 0, :, 1, q, :] = -sin
    wf_h, wf_l = split_np(wf.reshape(512, 256))
    return [wz_h, wz_l, ty, tx, fx, fy, wf_h, wf_l]


def split(a):
    hi = a.astype(BF)
    return hi, (a - hi.astype(F32)).astype(BF)


def dot(a, b):
    return jnp.dot(a, b, preferred_element_type=F32)


def apply_kernel(
    counts, vals, idx, pot, wz_h, wz_l, ty, tx, fx, fy, wf_h, wf_l, out,
    acc, ek, h, f, g, o,
):
    lane = lax.broadcasted_iota(jnp.int32, (1, 128), 1)
    turn = jnp.where(lane < 64, -1.0, 1.0).astype(F32)
    rows128 = lax.broadcasted_iota(jnp.int32, (128, 512), 0)
    rows256 = lax.broadcasted_iota(jnp.int32, (256, 512), 0)
    slot = lax.broadcasted_iota(jnp.int32, (1, 512), 1)

    acc[...] = jnp.zeros_like(acc)

    def place(i, _):
        cols, rows = [], []
        for q in range(4):
            k = i * 4 + q
            cell = idx[pl.ds(k, 1), :]
            wx = ((cell >> 12) + 16) & 63
            wy = ((cell >> 6) + 16) & 63
            wz = (cell + 16) & 63
            at_lane = (wx & 7) * 32 + wz
            at_row = (wx >> 3) * 32 + (wy & 3) * 8 + ((wy >> 2) & 7)
            live = slot < counts[k]
            cols.append(jnp.where(rows256 == at_lane, 1.0, 0.0).astype(BF))
            hit = rows128 == at_row
            parts = []
            for c in range(2):
                v = jnp.where(live, vals[k, pl.ds(c, 1), :], 0.0)
                for part in split(v):
                    parts.append(jnp.where(hit, part.astype(F32), 0.0).astype(BF))
            rows.append(jnp.concatenate(parts, axis=0))
        acc[...] += lax.dot_general(
            jnp.concatenate(rows, axis=1), jnp.concatenate(cols, axis=1),
            (((1,), (1,)), ((), ())), preferred_element_type=F32,
        )
        return 0

    lax.fori_loop(0, 8, place, 0)

    re = acc[0:128, :] + acc[128:256, :]
    im = acc[256:384, :] + acc[384:512, :]
    nrow = lax.broadcasted_iota(jnp.int32, (32, 128), 0)
    ny = ((nrow & 7) * 4 + (nrow >> 3) - 16).astype(F32)
    ksq = (8.0 / 4096.0) * ny * ny
    e = []
    for t in range(2):
        d = jnp.concatenate([re[:, t * 128 : t * 128 + 128], im[:, t * 128 : t * 128 + 128]], axis=1)
        dh, dl = split(d)
        e.append(dot(dh, wz_h[...]) + dot(dl, wz_h[...]) + dot(dh, wz_l[...]))

    def column(x):
        xh, t, q = x // 8, (x // 4) % 2, x % 4
        tile = e[t][xh * 32 : xh * 32 + 32, q * 128 : q * 128 + 128]
        bent = e[t][xh * 32 : xh * 32 + 32, 512 + q * 128 : 512 + q * 128 + 128]
        kin = (ksq + (8.0 / 4096.0) * (x - 16) ** 2) * tile + bent
        for j in range(4):
            ek[j, x * 8 : x * 8 + 8, :] = kin[j * 8 : j * 8 + 8, :]
        return jnp.concatenate([tile, turn * pltpu.roll(tile, 64, 1)], axis=0)

    for x in range(0, 32, 2):
        d = jnp.concatenate([column(x), column(x + 1)], axis=1)
        dh, dl = split(d)
        y = dot(ty[...], jnp.concatenate([dh, dl, dh], axis=0))
        h[x * HS : x * HS + 64, :] = y[:, 0:128]
        h[(x + 1) * HS : (x + 1) * HS + 64, :] = y[:, 128:256]

    def plane(i, _):
        both = []
        for q in range(2):
            tile = h[pl.ds(i * 2 + q, 32, stride=HS), :]
            both.append(jnp.concatenate([tile, turn * pltpu.roll(tile, 64, 1)], axis=0))
        dh, dl = split(jnp.concatenate(both, axis=1))
        real = dot(tx[...], jnp.concatenate([dh, dl, dh], axis=0))
        v = pot[i]
        vr = pltpu.roll(v, 64, 1)
        low = lane < 64
        vv = jnp.concatenate([jnp.where(low, v, vr), jnp.where(low, vr, v)], axis=1)
        dh, dl = split(real * vv)
        pq = dot(fx[...], jnp.concatenate([dh, dl, dh], axis=0))
        for q in range(2):
            p = pq[0:32, q * 128 : q * 128 + 128]
            s = pq[32:64, q * 128 : q * 128 + 128]
            start = pl.multiple_of((i * 2 + q) * FS, 8)
            f[pl.ds(start, 32), :] = p - turn * pltpu.roll(s, 64, 1)
        return 0

    lax.fori_loop(0, 32, plane, 0, unroll=4)

    def line(i, _):
        d = jnp.concatenate([f[pl.ds(i * 2 + q, 64, stride=FS), :] for q in range(2)], axis=1)
        dh, dl = split(d)
        pq = dot(fy[...], jnp.concatenate([dh, dl, dh], axis=0))
        for q in range(2):
            p = pq[0:32, q * 128 : q * 128 + 128]
            s = pq[32:64, q * 128 : q * 128 + 128]
            y = p - turn * pltpu.roll(s, 64, 1)
            start = pl.multiple_of((i * 2 + q) * 8, 8)
            for j in range(4):
                g[j, pl.ds(start, 8), :] = y[j * 8 : j * 8 + 8, :] + ek[j, pl.ds(start, 8), :]
        return 0

    lax.fori_loop(0, 16, line, 0, unroll=4)

    d = jnp.concatenate([g[j] for j in range(4)], axis=1)
    dh, dl = split(d)
    z = dot(dh, wf_h[...]) + dot(dl, wf_h[...]) + dot(dh, wf_l[...])
    for c in range(2):
        o[c] = z[:, c * 128 : c * 128 + 128]
        for b in range(8):
            out[0, c, :, b * 128 : b * 128 + 128] = o[c, pl.ds(b, 32, stride=8), :]


def apply_band(counts, vals, idx, pot):
    consts = tables()
    vm = pl.BlockSpec(memory_space=pltpu.VMEM)
    return pl.pallas_call(
        apply_kernel,
        out_shape=jax.ShapeDtypeStruct((1, 2, 32, 1024), F32),
        in_specs=[pl.BlockSpec(memory_space=pltpu.SMEM)] + [vm] * 11,
        out_specs=vm,
        scratch_shapes=[
            pltpu.VMEM((512, 256), F32),
            pltpu.VMEM((4, 256, 128), F32),
            pltpu.VMEM((32 * HS, 128), F32),
            pltpu.VMEM((64 * FS, 128), F32),
            pltpu.VMEM((4, 256, 128), F32),
            pltpu.VMEM((2, 256, 128), F32),
        ],
        compiler_params=pltpu.CompilerParams(vmem_limit_bytes=48 << 20),
        name="apply_band",
    )(counts, vals, idx, pot, *[jnp.asarray(c) for c in consts])

from jax.sharding import Mesh
from jax.sharding import PartitionSpec as P

GA = ("ga_0", "ga_1", "ga_2")
BAND = ("band_0", "band_1")
BAND_GA = ("band_0", "band_1", "ga_0", "ga_1", "ga_2")

def in_order(parts, dim):
    parts = jnp.moveaxis(parts, 0, dim)
    dims = parts.shape
    return parts.reshape(*dims[:dim], dims[dim] * dims[dim + 1], *dims[dim + 2 :])


def gather_in_order(value, axes, order):
    parts = value
    for k in order:
        parts = lax.all_gather(parts, axes[k])
    done = order[::-1]
    back = [done.index(k) for k in range(len(axes))]
    parts = parts.transpose(*back, *range(len(axes), parts.ndim))
    return parts.reshape(-1, *value.shape)


def gather_axes(value, axes, order, dim):
    return in_order(gather_in_order(value, axes, order), dim)


def cut_along(value, dim, peers):
    dims = value.shape
    parts = value.reshape(*dims[:dim], peers, dims[dim] // peers, *dims[dim + 1 :])
    return jnp.moveaxis(parts, dim, 0)


def sum_by_chip(value, chips, core, dim):
    sizes = (lax.axis_size(chips), lax.axis_size(core))
    parts = cut_along(value, dim, sizes[0] * sizes[1])
    inside = parts.shape[1:]
    parts = parts.reshape(*sizes, *inside).swapaxes(0, 1).reshape(-1, *inside)
    parts = lax.psum_scatter(parts, core, scatter_dimension=0, tiled=True)
    return lax.psum_scatter(parts, chips, scatter_dimension=0, tiled=True)[0]


def mixing(columns):
    real_cols = columns[0].T
    imag_cols = columns[1].T
    upper_rows = jnp.stack([real_cols, -imag_cols], axis=-1)
    lower_rows = jnp.stack([imag_cols, real_cols], axis=-1)
    stacked = jnp.stack([upper_rows, lower_rows], axis=1)
    return stacked.reshape(2 * real_cols.shape[0], 2 * real_cols.shape[1])


def per_device(coefficients, rotation, potential, index_map, counts):
    rot_full = gather_axes(rotation, GA, (2, 0, 1), 2)
    pot_full = gather_in_order(potential, GA, (2, 0, 1))
    band_local = coefficients.shape[0]
    slot_local = coefficients.shape[2]
    flat_coeffs = coefficients.reshape(2 * band_local, slot_local)
    product = jnp.dot(mixing(rot_full), flat_coeffs, precision=lax.Precision.HIGHEST)
    summed = sum_by_chip(
        product.reshape(rot_full.shape[2], 2, slot_local), "band_0", "band_1", 0
    )
    vals = lax.all_to_all(summed, GA, split_axis=0, concat_axis=0, tiled=True)
    return apply_band(counts, vals, index_map.reshape(32, 512), pot_full)


def solution(mesh):
    torus = Mesh(mesh.devices.reshape(4, 4, 2, 4, 2), ("ga_0", "ga_1", "ga_2", "band_0", "band_1"))
    placed = (P(BAND, None, GA), P(None, BAND, GA), P(None, GA), P(), P())
    return jax.shard_map(
        per_device,
        mesh=torus,
        in_specs=placed,
        out_specs=P(BAND_GA, None, None, None),
        check_vma=False,
    )
```

time: 274 us -> 147 us (0.54)
  other arithmetic: 96.3 us -> 0.1 us
  local copies, waits for them, and re-layouts: 47.1 us -> 14.3 us
  matrix products: 17.9 us -> 1.85 us
  Pallas kernels: 0 us -> 14.1 us
  waiting for transfers between devices: 27.4 us -> 31.6 us
    scatter-add x1 -> x0, other arithmetic: 94.4 us -> none  [apply_one(): jnp.zeros((2, window_cells), jnp.float32).at[:, window_index]]
    reshape x2 -> x1, local copies, waits for them, and re-layouts: 21.2 us -> 0.01 us  [per_device(): return apply_band(counts, vals, index_map.reshape(32, 512), pot_full)]
    dot_general x6 -> x0, matrix products: 16.1 us -> none  [the longest x2 7.08 us: transform(): jnp.einsum('dkcn,cnyz->dkyz', dft_table, grid_field, precision=lax.Precis...]
    pallas_call x0 -> x1, Pallas kernels: none -> 14.1 us  [apply_band(): pl.pallas_call(apply_kernel, out_shape=jax.ShapeDtypeStruct((1, 2, 32, 10...]
    mul x2 -> x0, local copies, waits for them, and re-layouts: 6.66 us -> none  [the longest x1 4.94 us: apply_one(): masked = values * live_mask[None, :]]
    dot_general x1 -> x0, local copies, waits for them, and re-layouts: 3 us -> none  [transform(): jnp.einsum('dkcn,cnyz->dkyz', dft_table, grid_field, precision=lax.Precis...]
  transfers between devices with their start and end apart: 4 -> 4, of which waited for: 4 -> 4; matrix products, arithmetic and copies ran while one was open for 3% -> 2% of each run, Pallas kernels for 0% -> 0%
where the time goes in v1:
time: 147 us
  blocking collectives  57 us (39%)
  waiting for transfers between devices  31.6 us (21%)
  between operations  15.1 us (10%)
  local copies, waits for them, and re-layouts  14.3 us (10%)
  Pallas kernels  14.1 us (10%)
  starting transfers between devices  12.6 us (9%)
  matrix products  1.85 us (1%)
    all_gather x5, blocking collectives, gather_in_order(): parts = lax.all_gather(parts, axes[k])  57 us
    reduce_scatter x1, waiting for transfers between devices, sum_by_chip(): parts = lax.psum_scatter(parts, core, scatter_dimension=0, tiled=True)  14.5 us
    pallas_call x1, Pallas kernels, apply_band(): pl.pallas_call(apply_kernel, out_shape=jax.ShapeDtypeStruct((1, 2, 32, 10...  14.1 us
    all_to_all x1, starting transfers between devices, per_device(): vals = lax.all_to_all(summed, GA, split_axis=0, concat_axis=0, tiled=True)  12.5 us
    all_gather x1, waiting for transfers between devices, gather_in_order(): parts = lax.all_gather(parts, axes[k])  8.3 us
    another operation x4, local copies, waits for them, and re-layouts, mixing(): stacked = jnp.stack([upper_rows, lower_rows], axis=1)  7.69 us
    reduce_scatter x1, waiting for transfers between devices, sum_by_chip(): return lax.psum_scatter(parts, chips, scatter_dimension=0, tiled=True)[0]  5.72 us
    all_to_all x1, waiting for transfers between devices, per_device(): vals = lax.all_to_all(summed, GA, split_axis=0, concat_axis=0, tiled=True)  3 us
  transfers between devices with their start and end apart: 4, of which 4 were waited for; matrix products, arithmetic and copies ran while one was open for 2% of the time, Pallas kernels for 0%

profile of v1, /device:TPU:32, one launch (start us, length us, event | category | flops | bytes accessed | tf_op | source)
XLA Modules:
  0.0 146.7 jit_solution(1120639058469491010)
XLA Ops:
  7.4 8.9 %all-gather = f32[4,256,8]{1,2,0:T(8,128)S(1)} all-gather(f32[2,256,8]{1,2,0:T(8,128)} %param.14), channel_id=2, replica_groups=mesh['ga_0'=4,'ga_1'=4,'ga_2'=2,'band_0'=4,'band_1'=2] {'ga_2'}, dimensions={0}, use_global_device_ids=true | all-gather | bytes 49152 | tf_op jit(solution)/shard_map/all_gather | solution.py:213
  16.3 12.5 %all-gather.1 = f32[8,2,256,8]{2,3,1,0:T(8,128)S(1)} all-gather(f32[2,2,256,8]{2,3,1,0:T(8,128)S(1)} %bitcast.53), channel_id=3, replica_groups=mesh['ga_0'=4,'ga_1'=4,'ga_2'=2,'band_0'=4,'band_1'=2] {'ga_0'}, dimensions={0}, use_global_device_ids=true | all-gather | bytes 163840 | tf_op jit(solution)/shard_map/all_gather | solution.py:213
  28.8 13.8 %all-gather.2 = f32[16,2,2,256,8]{3,4,2,1,0:T(8,128)S(1)} all-gather(f32[4,2,2,256,8]{3,4,2,1,0:T(8,128)S(1)} %bitcast.51), channel_id=4, replica_groups=mesh['ga_0'=4,'ga_1'=4,'ga_2'=2,'band_0'=4,'band_1'=2] {'ga_1'}, dimensions={0}, use_global_device_ids=true | all-gather | bytes 655360 | tf_op jit(solution)/shard_map/all_gather | solution.py:213
  42.7 0.1 pad_maximum_fusion
  42.8 0.2 copy.44
  43.0 1.9 %stack.28 = f32[4,2,32,1,512]{2,1,0,4,3:T(2,128)S(1)} reshape(f32[256,256,2]{0,2,1:T(2,128)S(1)} %copy.44) | data formatting | bytes 1048576 | tf_op jit(solution)/shard_map/stack | solution.py:244
  45.0 2.4 %copy.46 = f32[4,2,32,1,512]{4,2,3,1,0:T(8,128)} copy(f32[4,2,32,1,512]{2,1,0,4,3:T(2,128)S(1)} %stack.28) | data formatting | bytes 1048576 | tf_op jit(solution)/shard_map/stack | solution.py:244
  47.4 0.2 copy.45
  47.6 1.9 %stack.31 = f32[4,2,32,1,512]{2,1,0,4,3:T(2,128)S(1)} reshape(f32[256,256,2]{0,2,1:T(2,128)S(1)} %copy.45) | data formatting | bytes 1048576 | tf_op jit(solution)/shard_map/stack | solution.py:244
  49.6 1.4 copy.47
  51.0 1.9 %reshape.38 = f32[512,512,1,1,1]{1,0,2,3,4:T(8,128)S(1)} reshape(f32[256,2,512]{2,1,0:T(2,128)} %param.13) | data formatting | bytes 2097152 | tf_op jit(solution)/shard_map/reshape | solution.py:253
  53.0 1.8 %convolution_bitcast_fusion = f32[2,4,32,2,512]{4,2,3,0,1:T(8,128)S(1)} fusion(f32[4,2,32,1,512]{4,2,3,1,0:T(8,128)S(1)} %copy.47, f32[4,2,32,1,512]{4,2,3,1,0:T(8,128)S(1)} %copy-done.9, f32[512,512,1,1,1]{1,0,2,3,4:T(8,128)S(1)} %reshape.38), kind=kOutput, calls=%fused_computation | convolution fusion | flops 1610874880 | bytes 3145728 | tf_op jit(solution)/shard_map/dot_general | solution.py:254
  54.8 1.1 copy.48
  56.1 14.5 %reduce-scatter.3.cloned.1.call-done = f32[4,32,2,512]{3,1,2,0:T(8,128)} async-done(((f32[8,32,2,512]{3,1,2,0:T(8,128)}), f32[4,32,2,512]{3,1,2,0:T(8,128)}) %reduce-scatter.3.cloned.1.call-update) | async-done | bytes 524304 | tf_op jit(solution)/shard_map/reduce_scatter | solution.py:235
  70.7 0.0 all-gather.8.cloned.1.call-start
  70.7 8.5 %all-gather.3 = f32[128,128]{1,0:T(8,128)S(1)} all-gather(f32[64,128]{1,0:T(8,128)S(1)} %copy-done.11), channel_id=5, replica_groups=mesh['ga_0'=4,'ga_1'=4,'ga_2'=2,'band_0'=4,'band_1'=2] {'ga_2'}, dimensions={0}, use_global_device_ids=true | all-gather | bytes 98304 | tf_op jit(solution)/shard_map/all_gather | solution.py:213
  79.2 13.3 %all-gather.4 = f32[8,64,128]{2,1,0:T(8,128)} all-gather(f32[2,64,128]{2,1,0:T(8,128)S(1)} %bitcast.52), channel_id=6, replica_groups=mesh['ga_0'=4,'ga_1'=4,'ga_2'=2,'band_0'=4,'band_1'=2] {'ga_0'}, dimensions={0}, use_global_device_ids=true | all-gather | bytes 327680 | tf_op jit(solution)/shard_map/all_gather | solution.py:213
  92.6 5.7 %reduce-scatter.5.cloned.1.call-done = f32[1,32,2,512]{3,1,2,0:T(8,128)} async-done(((f32[4,32,2,512]{3,1,2,0:T(8,128)}), f32[1,32,2,512]{3,1,2,0:T(8,128)}) %reduce-scatter.5.cloned.1.call-update) | async-done | bytes 131088 | tf_op jit(solution)/shard_map/reduce_scatter | solution.py:236
  98.3 1.7 %copy.53 = f32[1,32,2,512]{3,2,1,0:T(2,128)} copy(f32[1,32,2,512]{3,1,2,0:T(8,128)} %reduce-scatter.5.cloned.1.call-done) | data formatting | bytes 262144 | tf_op jit(solution)/shard_map/reduce_scatter | solution.py:236
  100.0 12.5 %all-to-all-start = ((f32[32,2,512]{2,1,0:T(2,128)}), f32[32,2,512]{2,1,0:T(2,128)S(1)}, u32[]{:S(2)}, u32[]{:S(2)}) async-start(f32[32,2,512]{2,1,0:T(2,128)} %bitcast.43), calls=%async_computation.2 | async-start | bytes 262144 | tf_op jit(solution)/shard_map/all_to_all | solution.py:258
  112.5 8.3 %all-gather.8.cloned.1.call-done = f32[16,2,64,128]{3,2,1,0:T(8,128)} async-done(((f32[4,2,64,128]{3,2,1,0:T(8,128)}), f32[16,2,64,128]{3,2,1,0:T(8,128)}) %all-gather.8.cloned.1.call-update) | async-done | bytes 1048592 | tf_op jit(solution)/shard_map/all_gather | solution.py:213
  120.8 1.3 copy.50
  122.1 3.0 %all-to-all-done.vals = f32[32,2,512]{2,1,0:T(2,128)S(1)} async-done(((f32[32,2,512]{2,1,0:T(2,128)}), f32[32,2,512]{2,1,0:T(2,128)S(1)}, u32[]{:S(2)}, u32[]{:S(2)}) %all-to-all-start) | async-done | bytes 131104 | tf_op jit(solution)/shard_map/all_to_all | solution.py:258
  125.2 14.1 %apply_band.1 = f32[1,2,32,1024]{3,2,1,0:T(8,128)} custom-call(s32[32]{0:T(128)S(1)} %copy-done.8, f32[32,2,512]{2,1,0:T(2,128)S(1)} %all-to-all-done.vals, s32[32,512]{1,0:T(8,128)S(1)} %reshape.30.idx, f32[32,64,128]{2,1,0:T(8,128)S(1)} %bitcast.44, bf16[256,1024]{1,0:T(8,128)(2,1)S(1)} %copy-done, bf16[256,1024]{1,0:T(8,128)(2,1)S(1)} %copy-done.1, ...), custom_call_target="tpu_custom_call" | custom-call | tf_op jit(solution)/shard_map/apply_band/pallas_call | solution.py:180
  (33 shorter events, 0.3 us)
Async XLA Ops:
  7.4 63.3 %reduce-scatter.3.cloned.1.call-start = ((), (), s32[]{:S(2)}) async-start(), calls=%async_computation.3 | async-start | bytes 1572864 | tf_op jit(solution)/shard_map/reduce_scatter | solution.py:235
  49.5 3.4 %copy-start.9 = (f32[4,2,32,1,512]{4,2,3,1,0:T(8,128)S(1)}, f32[4,2,32,1,512]{4,2,3,1,0:T(8,128)}, u32[]{:S(2)}) copy-start(f32[4,2,32,1,512]{4,2,3,1,0:T(8,128)} %copy.46) | copy-start | bytes 1572868
  54.8 15.9 %copy-start.11 = (f32[64,128]{1,0:T(8,128)S(1)}, f32[64,128]{1,0:T(8,128)}, u32[]{:S(2)}) copy-start(f32[64,128]{1,0:T(8,128)} %param.15) | copy-start | bytes 98308
  54.8 57.6 %copy-start.10 = (s32[16384]{0:T(1024)S(1)}, s32[16384]{0:T(1024)}, u32[]{:S(2)}) copy-start(s32[16384]{0:T(1024)} %param.16) | copy-start | bytes 196612
  55.9 69.2 %copy-start = (bf16[256,1024]{1,0:T(8,128)(2,1)S(1)}, bf16[256,1024]{1,0:T(8,128)(2,1)}, u32[]{:S(2)}) copy-start(bf16[256,1024]{1,0:T(8,128)(2,1)} %constant.16.clone.wz_h) | copy-start | bytes 1572868
  56.0 69.1 %copy-start.1 = (bf16[256,1024]{1,0:T(8,128)(2,1)S(1)}, bf16[256,1024]{1,0:T(8,128)(2,1)}, u32[]{:S(2)}) copy-start(bf16[256,1024]{1,0:T(8,128)(2,1)} %constant.17.clone.wz_l) | copy-start | bytes 1572868
  56.0 69.1 %copy-start.2 = (bf16[512,256]{1,0:T(8,128)(2,1)S(1)}, bf16[512,256]{1,0:T(8,128)(2,1)}, u32[]{:S(2)}) copy-start(bf16[512,256]{1,0:T(8,128)(2,1)} %constant.22.clone.wf_h) | copy-start | bytes 786436
  56.0 69.1 %copy-start.3 = (bf16[512,256]{1,0:T(8,128)(2,1)S(1)}, bf16[512,256]{1,0:T(8,128)(2,1)}, u32[]{:S(2)}) copy-start(bf16[512,256]{1,0:T(8,128)(2,1)} %constant.23.clone.wf_l) | copy-start | bytes 786436
  56.0 69.1 %copy-start.4 = (bf16[64,192]{1,0:T(8,128)(2,1)S(1)}, bf16[64,192]{1,0:T(8,128)(2,1)}, u32[]{:S(2)}) copy-start(bf16[64,192]{1,0:T(8,128)(2,1)} %constant.18.clone.ty) | copy-start | bytes 73732
  56.0 69.1 %copy-start.5 = (bf16[64,192]{1,0:T(8,128)(2,1)S(1)}, bf16[64,192]{1,0:T(8,128)(2,1)}, u32[]{:S(2)}) copy-start(bf16[64,192]{1,0:T(8,128)(2,1)} %constant.19.clone.tx) | copy-start | bytes 73732
  56.0 69.1 %copy-start.6 = (bf16[64,192]{1,0:T(8,128)(2,1)S(1)}, bf16[64,192]{1,0:T(8,128)(2,1)}, u32[]{:S(2)}) copy-start(bf16[64,192]{1,0:T(8,128)(2,1)} %constant.20.clone.fx) | copy-start | bytes 73732
  56.0 69.1 %copy-start.7 = (bf16[64,192]{1,0:T(8,128)(2,1)S(1)}, bf16[64,192]{1,0:T(8,128)(2,1)}, u32[]{:S(2)}) copy-start(bf16[64,192]{1,0:T(8,128)(2,1)} %constant.21.clone.fy) | copy-start | bytes 73732
  56.0 69.1 %copy-start.8 = (s32[32]{0:T(128)S(1)}, s32[32]{0:T(128)}, u32[]{:S(2)}) copy-start(s32[32]{0:T(128)} %counts.1) | copy-start | bytes 388
  56.1 42.3 %reduce-scatter.5.cloned.1.call-start = ((), (), s32[]{:S(2)}) async-start(), calls=%async_computation.4 | async-start | bytes 655360 | tf_op jit(solution)/shard_map/reduce_scatter | solution.py:236
  70.7 50.1 %all-gather.8.cloned.1.call-start = ((), (), s32[]{:S(2)}) async-start(), calls=%async_computation.5 | async-start | bytes 1310720 | tf_op jit(solution)/shard_map/all_gather | solution.py:213
  100.0 25.1 %all-to-all-start = ((f32[32,2,512]{2,1,0:T(2,128)}), f32[32,2,512]{2,1,0:T(2,128)S(1)}, u32[]{:S(2)}, u32[]{:S(2)}) async-start(f32[32,2,512]{2,1,0:T(2,128)} %bitcast.43), calls=%async_computation.2 | async-start | bytes 262144 | tf_op jit(solution)/shard_map/all_to_all | solution.py:258
Sparse Core Ops, SparseCore 0:
  56.1 14.5 reduce-scatter.2
  73.2 25.0 reduce-scatter.4
Sparse Core Ops, SparseCore 1:
  92.7 28.1 all-gather.7

commit v2 on v1

--- a/solution.py
+++ b/solution.py
@@ -5,6 +5,8 @@
 from jax import lax
 from jax.experimental import pallas as pl
 from jax.experimental.pallas import tpu as pltpu
+from jax.sharding import Mesh
+from jax.sharding import PartitionSpec as P
 
 F32 = jnp.float32
 BF = jnp.bfloat16
@@ -89,7 +91,8 @@
             hit = rows128 == at_row
             parts = []
             for c in range(2):
-                v = jnp.where(live, vals[k, pl.ds(c, 1), :], 0.0)
+                row = jnp.concatenate([vals[k, pl.ds(c * 4 + t, 1), :] for t in range(4)], axis=1)
+                v = jnp.where(live, row, 0.0)
                 for part in split(v):
                     parts.append(jnp.where(hit, part.astype(F32), 0.0).astype(BF))
             rows.append(jnp.concatenate(parts, axis=0))
@@ -194,78 +197,251 @@
         name="apply_band",
     )(counts, vals, idx, pot, *[jnp.asarray(c) for c in consts])
 
-from jax.sharding import Mesh
-from jax.sharding import PartitionSpec as P
+
+MESH = pl.DeviceIdType.MESH
+
+
+def spread_kernel(
+    rot, pot, coef, vals, vg,
+    rg, ch, cl, sb, sr, pb, rz, ab,
+    r_send, r_recv, v_send, v_recv, s_send, s_recv, z_send, z_recv, a_send, a_recv, w_send, w_recv,
+):
+    y, x, zh = lax.axis_index("ga_0"), lax.axis_index("ga_1"), lax.axis_index("ga_2")
+    zl, core = lax.axis_index("band_0"), lax.axis_index("band_1")
+    xy = y * 4 + x
+    g = xy * 2 + zh
+    far = xy * 2 + (1 - zh)
+    half = pl.multiple_of(core * 32, 32)
+    other = {"ga_2": 1 - zh}
+    sibling = {"band_1": 1 - core}
+
+    def mate(i):
+        p = (xy + i) % 16
+        return p, {"ga_0": p // 4, "ga_1": p % 4}
+
+    barrier = pltpu.get_barrier_semaphore()
+
+    def greet(i, _):
+        pl.semaphore_signal(barrier, inc=1, device_id=mate(i)[1], device_id_type=MESH)
+        return 0
+
+    def hop(i, _):
+        pl.semaphore_signal(barrier, inc=1, device_id={"band_0": (zl + i) % 4}, device_id_type=MESH)
+        return 0
+
+    pl.semaphore_signal(barrier, inc=1, device_id=other, device_id_type=MESH)
+    lax.fori_loop(1, 16, greet, 0)
+    lax.fori_loop(1, 4, hop, 0)
+    pl.semaphore_signal(barrier, inc=1, device_id=sibling, device_id_type=MESH)
+    pl.semaphore_wait(barrier, 20)
+
+    def send(src, dst, send_sem, recv_sem, to):
+        return pltpu.make_async_remote_copy(
+            src_ref=src, dst_ref=dst, send_sem=send_sem, recv_sem=recv_sem,
+            device_id=to, device_id_type=MESH,
+        )
+
+    def rot_copy(block, i, src, to):
+        return send(src, rg.at[block], r_send.at[i], r_recv.at[block], to)
+
+    def pot_copy(block, i, src, to):
+        return send(src, vg.at[block, pl.ds(half, 32)], v_send.at[i], v_recv.at[block], to)
+
+    pot_src = pot.at[pl.ds(half, 32)]
+    rot_copy(g, 0, rot, other).start()
+
+    def rot_out(i, _):
+        rot_copy(g, i, rot, mate(i)[1]).start()
+        return 0
+
+    lax.fori_loop(1, 16, rot_out, 0)
+    pot_copy(g, 0, pot_src, other).start()
+
+    rg[g] = rot[...]
+    vg[g, pl.ds(half, 32), :] = pot[pl.ds(half, 32), :]
+
+    for c in range(2):
+        for t in range(4):
+            block = coef[pl.ds(t * 2 + c, 256, stride=8), :]
+            hi, lo = split(block)
+            ch[c * 256 : c * 256 + 256, t * 128 : t * 128 + 128] = hi
+            cl[c * 256 : c * 256 + 256, t * 128 : t * 128 + 128] = lo
+
+    rot_copy(far, 16, rg.at[far], other).wait_recv()
+
+    def rot_on(i, _):
+        rot_copy(far, 16 + i, rg.at[far], mate(i)[1]).start()
+        return 0
+
+    lax.fori_loop(1, 16, rot_on, 0)
+
+    def pot_out(i, _):
+        pot_copy(g, i, pot_src, mate(i)[1]).start()
+        return 0
+
+    lax.fori_loop(1, 16, pot_out, 0)
+    pot_far = vg.at[far, pl.ds(half, 32)]
+    pot_copy(far, 16, pot_far, other).wait_recv()
+
+    def pot_on(i, _):
+        pot_copy(far, 16 + i, pot_far, mate(i)[1]).start()
+        return 0
+
+    lax.fori_loop(1, 16, pot_on, 0)
+
+    def rot_in(i, _):
+        p, to = mate(i)
+        for h in range(2):
+            rot_copy(p * 2 + h, i, rot, to).wait_recv()
+        return 0
+
+    lax.fori_loop(1, 16, rot_in, 0)
+
+    def mixer(parity):
+        rows = []
+        for d in range(4):
+            for k in range(4):
+                block = (d * 2 + parity) * 4 + k
+                re, im = rg[block, 0], rg[block, 1]
+                rows.append(jnp.concatenate([re, -im], axis=1))
+                rows.append(jnp.concatenate([im, re], axis=1))
+        lh, ll = split(jnp.concatenate(rows, axis=0))
+        return dot(lh, ch[...]) + dot(ll, ch[...]) + dot(lh, cl[...])
+
+    def pair_copy(d):
+        return send(sb.at[d], sr.at[d], s_send.at[d], s_recv.at[d], sibling)
+
+    theirs = mixer(1 - core)
+    for d in range(4):
+        sb[d] = theirs[d * 64 : d * 64 + 64, :]
+    for d in range(4):
+        pair_copy(d).start()
+    mine = mixer(core)
+    for d in range(4):
+        pb[d] = mine[d * 64 : d * 64 + 64, :]
+    for d in range(4):
+        pair_copy(d).wait_recv()
+        pb[d] = pb[d] + sr[d]
+
+    def chip_copy(i):
+        d = (zl + i) % 4
+        return send(pb.at[d], rz.at[zl], z_send.at[i], z_recv.at[zl], {"band_0": d})
+
+    for i in range(1, 4):
+        chip_copy(i).start()
+    total = pb[zl]
+    for i in range(1, 4):
+        s = (zl + i) % 4
+        send(pb.at[s], rz.at[s], z_send.at[i], z_recv.at[s], {"band_0": s}).wait_recv()
+        total = total + rz[s]
+
+    for k in range(4):
+        for c in range(2):
+            for t in range(4):
+                piece = total[k * 16 + c * 8 : k * 16 + c * 8 + 8, t * 128 : t * 128 + 128]
+                ab[pl.ds(k * 64 + c * 4 + t, 8, stride=8), :] = piece
+
+    def band_copy(i):
+        p = (g + i) % 32
+        to = {"ga_0": p // 8, "ga_1": (p // 2) % 4, "ga_2": p % 2}
+        src = ab.at[pl.ds(pl.multiple_of(p * 8, 8), 8)]
+        return p, to, src
+
+    def band_out(i, _):
+        p, to, src = band_copy(i)
+        send(src, vals.at[g], a_send.at[i], a_recv.at[g], to).start()
+        return 0
+
+    lax.fori_loop(1, 32, band_out, 0)
+    vals[g] = ab[pl.ds(pl.multiple_of(g * 8, 8), 8), :]
+
+    def pot_in(i, _):
+        p, to = mate(i)
+        for h in range(2):
+            pot_copy(p * 2 + h, i, pot_src, to).wait_recv()
+        return 0
+
+    lax.fori_loop(1, 16, pot_in, 0)
+    swap = send(
+        vg.at[:, pl.ds(half, 32)], vg.at[:, pl.ds(half, 32)], w_send, w_recv, sibling
+    )
+    swap.start()
+
+    def rot_done(i, _):
+        to = mate(i)[1]
+        rot_copy(g, i, rot, to).wait_send()
+        rot_copy(far, 16 + i, rg.at[far], to).wait_send()
+        pot_copy(g, i, pot_src, to).wait_send()
+        pot_copy(far, 16 + i, pot_far, to).wait_send()
+        return 0
+
+    rot_copy(g, 0, rot, other).wait_send()
+    pot_copy(g, 0, pot_src, other).wait_send()
+    lax.fori_loop(1, 16, rot_done, 0)
+    for d in range(4):
+        pair_copy(d).wait_send()
+    for i in range(1, 4):
+        chip_copy(i).wait_send()
+
+    def band_in(i, _):
+        p, to, src = band_copy(i)
+        send(src, vals.at[p], a_send.at[i], a_recv.at[p], to).wait_recv()
+        return 0
+
+    def band_done(i, _):
+        p, to, src = band_copy(i)
+        send(src, vals.at[g], a_send.at[i], a_recv.at[g], to).wait_send()
+        return 0
+
+    lax.fori_loop(1, 32, band_in, 0)
+    lax.fori_loop(1, 32, band_done, 0)
+    swap.wait()
+
+
+def spread(rot, pot, coef):
+    vm = pl.BlockSpec(memory_space=pltpu.VMEM)
+    sems = [pltpu.SemaphoreType.DMA((n,)) for n in (32, 32, 32, 32, 4, 4, 4, 4, 32, 32)]
+    return pl.pallas_call(
+        spread_kernel,
+        out_shape=[
+            jax.ShapeDtypeStruct((32, 8, 128), F32),
+            jax.ShapeDtypeStruct((32, 64, 128), F32),
+        ],
+        in_specs=[vm] * 3,
+        out_specs=[vm] * 2,
+        scratch_shapes=[
+            pltpu.VMEM((32, 2, 8, 256), F32),
+            pltpu.VMEM((512, 512), BF),
+            pltpu.VMEM((512, 512), BF),
+            pltpu.VMEM((4, 64, 512), F32),
+            pltpu.VMEM((4, 64, 512), F32),
+            pltpu.VMEM((4, 64, 512), F32),
+            pltpu.VMEM((4, 64, 512), F32),
+            pltpu.VMEM((256, 128), F32),
+        ] + sems + [pltpu.SemaphoreType.DMA, pltpu.SemaphoreType.DMA],
+        compiler_params=pltpu.CompilerParams(
+            vmem_limit_bytes=32 << 20, collective_id=0, has_side_effects=True
+        ),
+        name="spread",
+    )(rot, pot, coef)
+
 
 GA = ("ga_0", "ga_1", "ga_2")
 BAND = ("band_0", "band_1")
-BAND_GA = ("band_0", "band_1", "ga_0", "ga_1", "ga_2")
-
-def in_order(parts, dim):
-    parts = jnp.moveaxis(parts, 0, dim)
-    dims = parts.shape
-    return parts.reshape(*dims[:dim], dims[dim] * dims[dim + 1], *dims[dim + 2 :])
-
-
-def gather_in_order(value, axes, order):
-    parts = value
-    for k in order:
-        parts = lax.all_gather(parts, axes[k])
-    done = order[::-1]
-    back = [done.index(k) for k in range(len(axes))]
-    parts = parts.transpose(*back, *range(len(axes), parts.ndim))
-    return parts.reshape(-1, *value.shape)
-
-
-def gather_axes(value, axes, order, dim):
-    return in_order(gather_in_order(value, axes, order), dim)
-
-
-def cut_along(value, dim, peers):
-    dims = value.shape
-    parts = value.reshape(*dims[:dim], peers, dims[dim] // peers, *dims[dim + 1 :])
-    return jnp.moveaxis(parts, dim, 0)
-
-
-def sum_by_chip(value, chips, core, dim):
-    sizes = (lax.axis_size(chips), lax.axis_size(core))
-    parts = cut_along(value, dim, sizes[0] * sizes[1])
-    inside = parts.shape[1:]
-    parts = parts.reshape(*sizes, *inside).swapaxes(0, 1).reshape(-1, *inside)
-    parts = lax.psum_scatter(parts, core, scatter_dimension=0, tiled=True)
-    return lax.psum_scatter(parts, chips, scatter_dimension=0, tiled=True)[0]
-
-
-def mixing(columns):
-    real_cols = columns[0].T
-    imag_cols = columns[1].T
-    upper_rows = jnp.stack([real_cols, -imag_cols], axis=-1)
-    lower_rows = jnp.stack([imag_cols, real_cols], axis=-1)
-    stacked = jnp.stack([upper_rows, lower_rows], axis=1)
-    return stacked.reshape(2 * real_cols.shape[0], 2 * real_cols.shape[1])
 
 
 def per_device(coefficients, rotation, potential, index_map, counts):
-    rot_full = gather_axes(rotation, GA, (2, 0, 1), 2)
-    pot_full = gather_in_order(potential, GA, (2, 0, 1))
-    band_local = coefficients.shape[0]
-    slot_local = coefficients.shape[2]
-    flat_coeffs = coefficients.reshape(2 * band_local, slot_local)
-    product = jnp.dot(mixing(rot_full), flat_coeffs, precision=lax.Precision.HIGHEST)
-    summed = sum_by_chip(
-        product.reshape(rot_full.shape[2], 2, slot_local), "band_0", "band_1", 0
-    )
-    vals = lax.all_to_all(summed, GA, split_axis=0, concat_axis=0, tiled=True)
-    return apply_band(counts, vals, index_map.reshape(32, 512), pot_full)
+    coef = coefficients.reshape(256, 2, 4, 128).transpose(0, 2, 1, 3).reshape(2048, 128)
+    vals, pot = spread(rotation.transpose(0, 2, 1), potential, coef)
+    return apply_band(counts, vals, index_map.reshape(32, 512), pot)
 
 
 def solution(mesh):
-    torus = Mesh(mesh.devices.reshape(4, 4, 2, 4, 2), ("ga_0", "ga_1", "ga_2", "band_0", "band_1"))
-    placed = (P(BAND, None, GA), P(None, BAND, GA), P(None, GA), P(), P())
+    torus = Mesh(mesh.devices.reshape(4, 4, 2, 4, 2), GA + BAND)
     return jax.shard_map(
         per_device,
         mesh=torus,
-        in_specs=placed,
-        out_specs=P(BAND_GA, None, None, None),
+        in_specs=(P(BAND, None, GA), P(None, BAND, GA), P(None, GA), P(), P()),
+        out_specs=P(BAND + GA, None, None, None),
         check_vma=False,
     )

time: 147 us -> 65.1 us (0.44)
  blocking collectives: 57 us -> 0 us
  Pallas kernels: 14.1 us -> 58.7 us
  waiting for transfers between devices: 31.6 us -> 0 us
  between operations: 15.1 us -> 0.1 us
  starting transfers between devices: 12.6 us -> 0 us
  local copies, waits for them, and re-layouts: 14.3 us -> 5.34 us
  matrix products: 1.85 us -> 0 us
    all_gather x5 -> x0, blocking collectives: 57 us -> none  [gather_in_order(): parts = lax.all_gather(parts, axes[k])]
    pallas_call x0 -> x1, Pallas kernels: none -> 44.6 us  [spread(): pl.pallas_call(spread_kernel, out_shape=[jax.ShapeDtypeStruct((32, 8, 128...]
    reduce_scatter x2 -> x0, waiting for transfers between devices: 20.3 us -> none  [the longest x1 14.5 us: sum_by_chip(): parts = lax.psum_scatter(parts, core, scatter_dimension=0, tiled=True)]
    all_to_all x1 -> x0, starting transfers between devices: 12.5 us -> none  [per_device(): vals = lax.all_to_all(summed, GA, split_axis=0, concat_axis=0, tiled=True)]
    all_gather x1 -> x0, waiting for transfers between devices: 8.3 us -> none  [gather_in_order(): parts = lax.all_gather(parts, axes[k])]
    another operation x7 -> x0, local copies, waits for them, and re-layouts: 8.18 us -> none  [the longest x4 7.69 us: mixing(): stacked = jnp.stack([upper_rows, lower_rows], axis=1)]
    unnamed x24, local copies, waits for them, and re-layouts: 0.08 us -> 4.46 us
    all_to_all x1 -> x0, waiting for transfers between devices: 3 us -> none  [per_device(): vals = lax.all_to_all(summed, GA, split_axis=0, concat_axis=0, tiled=True)]
  transfers between devices with their start and end apart: 4 -> 0, of which waited for: 4 -> 0; matrix products, arithmetic and copies ran while one was open for 2% -> 0% of each run, Pallas kernels for 0% -> 0%
where the time goes in v2:
time: 65.1 us; the launch traced here: 64.1 us
  Pallas kernels  58.7 us (90%)
  local copies, waits for them, and re-layouts  5.34 us (8%)
    pallas_call x1, Pallas kernels, spread(): pl.pallas_call(spread_kernel, out_shape=[jax.ShapeDtypeStruct((32, 8, 128...  44.6 us
    pallas_call x1, Pallas kernels, apply_band(): pl.pallas_call(apply_kernel, out_shape=jax.ShapeDtypeStruct((1, 2, 32, 10...  14.1 us
    unnamed x24, local copies, waits for them, and re-layouts  4.46 us

profile of v2, /device:TPU:32, one launch (start us, length us, event | category | flops | bytes accessed | tf_op | source)
XLA Modules:
  0.0 64.1 jit_solution(9535266640424702239)
XLA Ops:
  0.0 0.0 copy-start.9
  0.0 0.0 copy-start.6
  0.0 0.0 copy-start.7
  0.0 0.0 copy-start.8
  0.0 0.9 %reshape.11.idx = s32[32,512]{1,0:T(8,128)S(1)} reshape(s32[16384]{0:T(1024)} %param.16) | data formatting | bytes 131072 | tf_op jit(solution)/shard_map/reshape | solution.py:436
  0.9 0.0 copy-done.9
  0.9 0.0 copy-start
  0.9 1.2 %copy-done = f32[256,2,512]{2,1,0:T(2,128)S(1)} copy-done((f32[256,2,512]{2,1,0:T(2,128)S(1)}, f32[256,2,512]{2,1,0:T(2,128)}, u32[]{:S(2)}) %copy-start) | copy-done | bytes 1048600
  2.1 0.0 copy-start.10
  2.1 0.7 %copy-done.10 = f32[2,256,8]{1,2,0:T(8,128)S(1)} copy-done((f32[2,256,8]{1,2,0:T(8,128)S(1)}, f32[2,256,8]{1,2,0:T(8,128)}, u32[]{:S(2)}) %copy-start.10) | copy-done | bytes 16408
  2.9 0.0 copy-start.1
  2.9 0.0 copy-start.2
  2.9 44.6 %spread.1 = (f32[32,8,128]{2,1,0:T(8,128)S(1)}, f32[32,64,128]{2,1,0:T(8,128)S(1)}) custom-call(f32[2,8,256]{2,1,0:T(8,128)S(1)} %bitcast.7, f32[64,128]{1,0:T(8,128)S(1)} %copy-done.9, f32[2048,128]{1,0:T(8,128)S(1)} %bitcast.6), custom_call_target="tpu_custom_call" | custom-call | tf_op jit(solution)/shard_map/spread/pallas_call | solution.py:404
  47.5 0.0 copy-start.11
  47.5 0.0 copy-done.6
  47.5 0.0 copy-done.7
  47.5 0.0 copy-done.8
  47.5 0.0 copy-done.1
  47.5 0.0 copy-done.2
  47.5 0.0 copy-done.5
  47.5 0.6 copy-done.11
  48.1 0.9 %copy-done.3 = bf16[512,256]{1,0:T(8,128)(2,1)S(1)} copy-done((bf16[512,256]{1,0:T(8,128)(2,1)S(1)}, bf16[512,256]{1,0:T(8,128)(2,1)}, u32[]{:S(2)}) %copy-start.3) | copy-done | bytes 262168
  49.1 0.9 %copy-done.4 = bf16[512,256]{1,0:T(8,128)(2,1)S(1)} copy-done((bf16[512,256]{1,0:T(8,128)(2,1)S(1)}, bf16[512,256]{1,0:T(8,128)(2,1)}, u32[]{:S(2)}) %copy-start.4) | copy-done | bytes 262168
  50.0 14.1 %apply_band.1 = f32[1,2,32,1024]{3,2,1,0:T(8,128)} custom-call(s32[32]{0:T(128)S(1)} %copy-done.11, f32[32,8,128]{2,1,0:T(8,128)S(1)} %get-tuple-element.7.vals, s32[32,512]{1,0:T(8,128)S(1)} %reshape.11.idx, f32[32,64,128]{2,1,0:T(8,128)S(1)} %get-tuple-element.8.pot, bf16[256,1024]{1,0:T(8,128)(2,1)S(1)} %copy-done.2, bf16[256,1024]{1,0:T(8,128)(2,1)S(1)} %copy-done.1, ...), custom_call_target="tpu_custom_call" | custom-call | tf_op jit(solution)/shard_map/apply_band/pallas_call | solution.py:183
  (3 shorter events, 0.0 us)
Async XLA Ops:
  0.0 0.9 %copy-start.9 = (f32[64,128]{1,0:T(8,128)S(1)}, f32[64,128]{1,0:T(8,128)}, u32[]{:S(2)}) copy-start(f32[64,128]{1,0:T(8,128)} %pot.1) | copy-start | bytes 98308
  0.0 47.5 %copy-start.6 = (bf16[64,192]{1,0:T(8,128)(2,1)S(1)}, bf16[64,192]{1,0:T(8,128)(2,1)}, u32[]{:S(2)}) copy-start(bf16[64,192]{1,0:T(8,128)(2,1)} %constant.20.clone.fx) | copy-start | bytes 73732
  0.0 47.5 %copy-start.7 = (bf16[64,192]{1,0:T(8,128)(2,1)S(1)}, bf16[64,192]{1,0:T(8,128)(2,1)}, u32[]{:S(2)}) copy-start(bf16[64,192]{1,0:T(8,128)(2,1)} %constant.19.clone.tx) | copy-start | bytes 73732
  0.0 47.5 %copy-start.8 = (bf16[64,192]{1,0:T(8,128)(2,1)S(1)}, bf16[64,192]{1,0:T(8,128)(2,1)}, u32[]{:S(2)}) copy-start(bf16[64,192]{1,0:T(8,128)(2,1)} %constant.18.clone.ty) | copy-start | bytes 73732
  0.9 1.2 %copy-start = (f32[256,2,512]{2,1,0:T(2,128)S(1)}, f32[256,2,512]{2,1,0:T(2,128)}, u32[]{:S(2)}) copy-start(f32[256,2,512]{2,1,0:T(2,128)} %param.13) | copy-start | bytes 3145732
  2.1 0.7 %copy-start.10 = (f32[2,256,8]{1,2,0:T(8,128)S(1)}, f32[2,256,8]{1,2,0:T(8,128)}, u32[]{:S(2)}) copy-start(f32[2,256,8]{1,2,0:T(8,128)} %param.14) | copy-start | bytes 49156
  2.9 44.6 %copy-start.1 = (bf16[256,1024]{1,0:T(8,128)(2,1)S(1)}, bf16[256,1024]{1,0:T(8,128)(2,1)}, u32[]{:S(2)}) copy-start(bf16[256,1024]{1,0:T(8,128)(2,1)} %constant.17.clone.wz_l) | copy-start | bytes 1572868
  2.9 44.7 %copy-start.2 = (bf16[256,1024]{1,0:T(8,128)(2,1)S(1)}, bf16[256,1024]{1,0:T(8,128)(2,1)}, u32[]{:S(2)}) copy-start(bf16[256,1024]{1,0:T(8,128)(2,1)} %constant.16.clone.wz_h) | copy-start | bytes 1572868
  2.9 44.7 %copy-start.5 = (bf16[64,192]{1,0:T(8,128)(2,1)S(1)}, bf16[64,192]{1,0:T(8,128)(2,1)}, u32[]{:S(2)}) copy-start(bf16[64,192]{1,0:T(8,128)(2,1)} %constant.21.clone.fy) | copy-start | bytes 73732
  47.5 0.7 %copy-start.11 = (s32[32]{0:T(128)S(1)}, s32[32]{0:T(128)}, u32[]{:S(2)}) copy-start(s32[32]{0:T(128)} %counts.1) | copy-start | bytes 388
  48.1 0.9 %copy-start.3 = (bf16[512,256]{1,0:T(8,128)(2,1)S(1)}, bf16[512,256]{1,0:T(8,128)(2,1)}, u32[]{:S(2)}) copy-start(bf16[512,256]{1,0:T(8,128)(2,1)} %constant.23.clone.wf_l) | copy-start | bytes 786436
  49.1 0.9 %copy-start.4 = (bf16[512,256]{1,0:T(8,128)(2,1)S(1)}, bf16[512,256]{1,0:T(8,128)(2,1)}, u32[]{:S(2)}) copy-start(bf16[512,256]{1,0:T(8,128)(2,1)} %constant.22.clone.wf_h) | copy-start | bytes 786436

commit v3 on v1

v3 whole, which is shorter than its diff:
```python
import math

import jax
import jax.numpy as jnp
import numpy as np
from jax import lax
from jax.experimental import pallas as pl
from jax.experimental.pallas import tpu as pltpu
from jax.sharding import Mesh
from jax.sharding import PartitionSpec as P

F32 = jnp.float32
BF = jnp.bfloat16
MESH = pl.DeviceIdType.MESH
GA = ("ga_0", "ga_1", "ga_2")
BAND = ("band_0", "band_1")
HS = 72
FS = 40
EARLY = 12


def split_np(a):
    a = np.asarray(a, np.float32)
    hi = a.astype(BF)
    lo = (a - hi.astype(np.float32)).astype(BF)
    return hi, lo


def stack3(a):
    hi, lo = split_np(a)
    return np.concatenate([hi, hi, lo], axis=1)


def tables():
    n = np.arange(32) - 16
    r = np.arange(64)
    ang = 2.0 * math.pi * ((r[:, None] * n[None, :]) % 64) / 64.0
    cos, sin = np.cos(ang), np.sin(ang)
    perm = np.array([(k % 8) * 4 + k // 8 for k in range(32)])
    s = 8.0 / 4096.0
    wz = np.zeros((2, 4, 32, 2, 4, 2, 64))
    for q in range(4):
        wz[0, q, :, 0, q, 0, :] = cos.T / 64
        wz[1, q, :, 0, q, 0, :] = -sin.T / 64
        wz[0, q, :, 0, q, 1, :] = sin.T / 64
        wz[1, q, :, 0, q, 1, :] = cos.T / 64
    wz[:, :, :, 1] = wz[:, :, :, 0] * (s * n * n)[None, None, :, None, None, None]
    wz_h, wz_l = split_np(wz.reshape(256, 1024))
    ty = stack3(np.concatenate([cos[:, perm], sin[:, perm]], axis=1) / 64)
    tx = stack3(np.concatenate([cos, sin], axis=1) / 64)
    fx = stack3(np.concatenate([cos.T, sin.T], axis=0))
    fy = stack3(np.concatenate([cos.T[perm], sin.T[perm]], axis=0))
    wf = np.zeros((4, 2, 64, 2, 4, 32))
    for q in range(4):
        wf[q, 0, :, 0, q, :] = cos
        wf[q, 1, :, 0, q, :] = sin
        wf[q, 1, :, 1, q, :] = cos
        wf[q, 0, :, 1, q, :] = -sin
    wf_h, wf_l = split_np(wf.reshape(512, 256))
    return [wz_h, wz_l, ty, tx, fx, fy, wf_h, wf_l]


def split(a):
    hi = a.astype(BF)
    return hi, (a - hi.astype(F32)).astype(BF)


def dot(a, b):
    return jnp.dot(a, b, preferred_element_type=F32)


def kernel(
    rot_in, pot_in, coef_in, idx_in, counts_in,
    wz_h_in, wz_l_in, ty_in, tx_in, fx_in, fy_in, wf_h_in, wf_l_in,
    out,
    rot, pot, coef, idx, counts, wz_h, wz_l, ty, tx, fx, fy, wf_h, wf_l,
    rg, vg, ch, cl, sb, sr, pb, rz, ab, vals, cols, rows, acc, ek, h, f, gz, o,
    l_sem, r_send, r_recv, v_send, v_recv, s_send, s_recv, z_send, z_recv,
    a_send, a_recv, w_send, w_recv,
):
    y, x, zh = lax.axis_index("ga_0"), lax.axis_index("ga_1"), lax.axis_index("ga_2")
    zl, core = lax.axis_index("band_0"), lax.axis_index("band_1")
    g = y * 8 + x * 2 + zh
    far = y * 8 + x * 2 + (1 - zh)
    half = pl.multiple_of(core * 32, 32)
    other = {"ga_2": 1 - zh}
    sibling = {"band_1": 1 - core}

    local = [
        pltpu.make_async_copy(a, b, l_sem.at[n])
        for n, (a, b) in enumerate([
            (rot_in.at[:, :, 0:128], rot.at[0]), (coef_in, coef), (pot_in, pot), (idx_in, idx),
            (counts_in, counts), (wz_h_in, wz_h), (wz_l_in, wz_l), (ty_in, ty),
            (tx_in, tx), (fx_in, fx), (fy_in, fy), (wf_h_in, wf_h), (wf_l_in, wf_l),
            (rot_in.at[:, :, 128:256], rot.at[1]),
        ])
    ]
    for n in (0, 13, *range(1, 13)):
        local[n].start()

    def mate(i):
        a, b = i // 4, i % 4
        yy = (y + (a ^ (a >> 1))) % 4
        xx = (x + (b ^ (b >> 1))) % 4
        return yy * 4 + xx, {"ga_0": yy, "ga_1": xx}

    barrier = pltpu.get_barrier_semaphore()

    def greet(i, _):
        pl.semaphore_signal(barrier, inc=1, device_id=mate(i)[1], device_id_type=MESH)
        return 0

    def hop(i, _):
        pl.semaphore_signal(barrier, inc=1, device_id={"band_0": (zl + i) % 4}, device_id_type=MESH)
        return 0

    pl.semaphore_signal(barrier, inc=1, device_id=other, device_id_type=MESH)
    lax.fori_loop(1, 16, greet, 0)
    lax.fori_loop(1, 4, hop, 0)
    pl.semaphore_signal(barrier, inc=1, device_id=sibling, device_id_type=MESH)

    local[0].wait()
    local[13].wait()
    for t in range(2):
        for s in range(2):
            for r in range(2):
                rg[g, s, r * 4 : r * 4 + 4, t * 128 : t * 128 + 128] = rot[
                    t, r, pl.ds(s, 4, stride=2), :
                ]
    local[2].wait()
    vg[g, pl.ds(half, 32), :] = pot[pl.ds(half, 32), :]
    pl.semaphore_wait(barrier, 20)

    def send(src, dst, send_sem, recv_sem, to):
        return pltpu.make_async_remote_copy(
            src_ref=src, dst_ref=dst, send_sem=send_sem, recv_sem=recv_sem,
            device_id=to, device_id_type=MESH,
        )

    def rot_copy(block, i, to):
        return send(rg.at[block], rg.at[block], r_send.at[i], r_recv.at[block], to)

    def pot_copy(block, i, to):
        piece = vg.at[block, pl.ds(half, 32)]
        return send(piece, piece, v_send.at[i], v_recv.at[block], to)

    def each(lo, copy):
        def step(i, _):
            copy(i).start()
            return 0

        lax.fori_loop(lo, 16, step, 0)

    rot_copy(g, 0, other).start()
    each(1, lambda i: rot_copy(g, i, mate(i)[1]))
    pot_copy(g, 0, other).start()

    local[1].wait()
    for c in range(2):
        for t in range(4):
            hi, lo = split(coef[pl.ds(t * 2 + c, 256, stride=8), :])
            ch[c * 256 : c * 256 + 256, t * 128 : t * 128 + 128] = hi
            cl[c * 256 : c * 256 + 256, t * 128 : t * 128 + 128] = lo

    local[3].wait()
    local[4].wait()
    rows128 = lax.broadcasted_iota(jnp.int32, (128, 512), 0)
    rows256 = lax.broadcasted_iota(jnp.int32, (256, 512), 0)
    slot = lax.broadcasted_iota(jnp.int32, (1, 512), 1)

    def one_hot(k, _):
        cell = jnp.concatenate([idx[pl.ds(k * 4 + t, 1), :] for t in range(4)], axis=1)
        wx = ((cell >> 12) + 16) & 63
        wy = ((cell >> 6) + 16) & 63
        wz = (cell + 16) & 63
        at_lane = (wx & 7) * 32 + wz
        at_row = (wx >> 3) * 32 + (wy & 3) * 8 + ((wy >> 2) & 7)
        at_row = jnp.where(slot < counts[k], at_row, -1)
        cols[k] = jnp.where(rows256 == at_lane, 1.0, 0.0).astype(BF)
        rows[k] = jnp.where(rows128 == at_row, 1.0, 0.0).astype(BF)
        return 0

    lax.fori_loop(0, EARLY, one_hot, 0)

    rot_copy(far, 16, other).wait_recv()
    each(1, lambda i: rot_copy(far, 16 + i, mate(i)[1]))
    each(1, lambda i: pot_copy(g, i, mate(i)[1]))
    pot_copy(far, 16, other).wait_recv()
    each(1, lambda i: pot_copy(far, 16 + i, mate(i)[1]))

    lax.fori_loop(EARLY, 32, one_hot, 0)

    sub = lax.broadcasted_iota(jnp.int32, (8, 256), 0)
    flip = jnp.where(sub < 4, -1.0, 1.0).astype(F32)

    def pair_copy(d):
        return send(sb.at[d], sr.at[d], s_send.at[d], s_recv.at[d], sibling)

    def chip_copy(d, part, to, place):
        return send(
            pb.at[d, pl.ds(part * 32, 32)], rz.at[part, place],
            z_send.at[part * 4 + d], z_recv.at[part * 5 + place], {"band_0": to},
        )

    def mix(n):
        d = (y + (n ^ (n >> 1))) % 4

        def rot_wait(i, _):
            p, to = mate(i)
            rot_copy(p * 2, 0, to).wait_recv()
            rot_copy(p * 2 + 1, 0, to).wait_recv()
            return 0

        lax.fori_loop(max(1, n * 4), n * 4 + 4, rot_wait, 0)
        left, right = [], []
        for parity in (1 - core, core):
            for s in (1 - zh, zh):
                for k in range(4):
                    block = rg[d * 8 + parity * 4 + k, s]
                    left.append(block)
                    right.append(flip * pltpu.roll(block, 4, 0))
        lh, ll = split(jnp.concatenate([jnp.concatenate(left, 0), jnp.concatenate(right, 0)], 1))
        both = dot(lh, ch[...]) + dot(ll, ch[...]) + dot(lh, cl[...])
        sb[d] = both[0:64]
        pb[d] = both[64:128]
        pair_copy(d).start()

    def scatter_half(n, part):
        d = (y + (n ^ (n >> 1))) % 4
        up = (zl == 0) & (d == 2)
        down = (zl == 3) & (d == 1)
        wait_for = ((zl == 1) & (d == 2)) | ((zl == 2) & (d == 1))

        @pl.when((d != zl) & jnp.logical_not(wait_for))
        def _():
            to = jnp.where(up, 1, jnp.where(down, 2, d))
            place = jnp.where(up | down, 4, zl)
            chip_copy(d, part, to, place).start()

    def settle(n):
        d = (y + (n ^ (n >> 1))) % 4
        pair_copy(d).wait_recv()
        pb[d] = pb[d] + sr[d]
        scatter_half(n, 0)

    mix(0)
    for n in range(1, 4):
        mix(n)
        settle(n - 1)
    settle(3)

    def merge(part):
        @pl.when((zl == 1) | (zl == 2))
        def _():
            d = 3 - zl
            chip_copy(d, part, d, 4).wait_recv()
            pb[d, part * 32 : part * 32 + 32] = pb[d, part * 32 : part * 32 + 32] + rz[part, 4]
            chip_copy(d, part, d, zl).start()

    def band_copy(p, part, to):
        s = (1 - zh) if part == 0 else zh
        gg = p * 2 + s
        src = ab.at[pl.ds(pl.multiple_of(gg * 8, 8), 8)]
        return send(src, vals.at[g], a_send.at[gg], a_recv.at[g], {**to, "ga_2": s})

    def finish(part):
        s = (1 - zh) if part == 0 else zh
        for src in range(4):
            skip = (zl == src) | ((zl == 2) & (src == 0)) | ((zl == 1) & (src == 3))

            @pl.when(jnp.logical_not(skip))
            def _():
                chip_copy(zl, part, zl, src).wait_recv()
                pb[zl, part * 32 : part * 32 + 32] = (
                    pb[zl, part * 32 : part * 32 + 32] + rz[part, src]
                )

        total = pb[zl, part * 32 : part * 32 + 32]
        for k in range(4):
            for c in range(2):
                for t in range(4):
                    piece = total[k * 8 + c * 4 : k * 8 + c * 4 + 4, t * 128 : t * 128 + 128]
                    ab[pl.ds(k * 64 + s * 8 + c * 4 + t, 4, stride=16), :] = piece

        def out_step(i, _):
            p, to = mate(15 - i)
            band_copy(p, part, to).start()
            return 0

        lax.fori_loop(0, 16 - part, out_step, 0)

    merge(0)
    for n in range(4):
        scatter_half(n, 1)
    finish(0)
    merge(1)
    finish(1)
    vals[g] = ab[pl.ds(pl.multiple_of(g * 8, 8), 8), :]

    def pot_wait(i, _):
        p, to = mate(i)
        pot_copy(p * 2, 0, to).wait_recv()
        pot_copy(p * 2 + 1, 0, to).wait_recv()
        return 0

    lax.fori_loop(1, 16, pot_wait, 0)
    side = vg.at[:, pl.ds(half, 32)]
    swap = send(side, side, w_send, w_recv, sibling)
    swap.start()

    def place(i, first=False):
        p, to = mate(i)
        if first:
            send(ab.at[pl.ds(0, 8)], vals.at[far], a_send.at[0], a_recv.at[far], to).wait_recv()
        else:
            for q in range(2):
                k = p * 2 + q
                send(ab.at[pl.ds(0, 8)], vals.at[k], a_send.at[0], a_recv.at[k], to).wait_recv()
        left = []
        for q in range(2):
            k = p * 2 + q
            hit = rows[k]
            parts = []
            for c in range(2):
                v = jnp.concatenate([vals[k, pl.ds(c * 4 + t, 1), :] for t in range(4)], axis=1)
                high = v.astype(BF).astype(F32)
                for part in (high, v - high):
                    wide = jnp.broadcast_to(part, (16, 512)).astype(BF)
                    parts.append(hit * jnp.concatenate([wide] * 8, axis=0))
            left.append(jnp.concatenate(parts, axis=0))
        right = jnp.concatenate([cols[p * 2], cols[p * 2 + 1]], axis=1)
        placed = lax.dot_general(
            jnp.concatenate(left, axis=1), right, (((1,), (1,)), ((), ())),
            preferred_element_type=F32,
        )
        if first:
            acc[...] = placed
        else:
            acc[...] += placed

    place(0, True)

    def place_step(i, _):
        place(i)
        return 0

    lax.fori_loop(1, 16, place_step, 0)

    for copy in local[5:13]:
        copy.wait()
    lane = lax.broadcasted_iota(jnp.int32, (1, 128), 1)
    turn = jnp.where(lane < 64, -1.0, 1.0).astype(F32)
    re = acc[0:128, :] + acc[128:256, :]
    im = acc[256:384, :] + acc[384:512, :]
    nrow = lax.broadcasted_iota(jnp.int32, (32, 128), 0)
    ny = ((nrow & 7) * 4 + (nrow >> 3) - 16).astype(F32)
    ksq = (8.0 / 4096.0) * ny * ny
    e = []
    for t in range(2):
        d = jnp.concatenate([re[:, t * 128 : t * 128 + 128], im[:, t * 128 : t * 128 + 128]], axis=1)
        dh, dl = split(d)
        e.append(dot(dh, wz_h[...]) + dot(dl, wz_h[...]) + dot(dh, wz_l[...]))

    def column(i):
        xh, t, q = i // 8, (i // 4) % 2, i % 4
        tile = e[t][xh * 32 : xh * 32 + 32, q * 128 : q * 128 + 128]
        bent = e[t][xh * 32 : xh * 32 + 32, 512 + q * 128 : 512 + q * 128 + 128]
        kin = (ksq + (8.0 / 4096.0) * (i - 16) ** 2) * tile + bent
        for j in range(4):
            ek[j, i * 8 : i * 8 + 8, :] = kin[j * 8 : j * 8 + 8, :]
        return jnp.concatenate([tile, turn * pltpu.roll(tile, 64, 1)], axis=0)

    for i in range(0, 32, 2):
        dh, dl = split(jnp.concatenate([column(i), column(i + 1)], axis=1))
        d = dot(ty[...], jnp.concatenate([dh, dl, dh], axis=0))
        h[i * HS : i * HS + 64, :] = d[:, 0:128]
        h[(i + 1) * HS : (i + 1) * HS + 64, :] = d[:, 128:256]

    swap.wait()

    def plane(i, _):
        both = []
        for q in range(2):
            tile = h[pl.ds(i * 2 + q, 32, stride=HS), :]
            both.append(jnp.concatenate([tile, turn * pltpu.roll(tile, 64, 1)], axis=0))
        dh, dl = split(jnp.concatenate(both, axis=1))
        real = dot(tx[...], jnp.concatenate([dh, dl, dh], axis=0))
        v = vg[i]
        vr = pltpu.roll(v, 64, 1)
        low = lane < 64
        vv = jnp.concatenate([jnp.where(low, v, vr), jnp.where(low, vr, v)], axis=1)
        dh, dl = split(real * vv)
        pq = dot(fx[...], jnp.concatenate([dh, dl, dh], axis=0))
        for q in range(2):
            pp = pq[0:32, q * 128 : q * 128 + 128]
            qq = pq[32:64, q * 128 : q * 128 + 128]
            start = pl.multiple_of((i * 2 + q) * FS, 8)
            f[pl.ds(start, 32), :] = pp - turn * pltpu.roll(qq, 64, 1)
        return 0

    lax.fori_loop(0, 32, plane, 0, unroll=16)

    def line(i, _):
        d = jnp.concatenate([f[pl.ds(i * 2 + q, 64, stride=FS), :] for q in range(2)], axis=1)
        dh, dl = split(d)
        pq = dot(fy[...], jnp.concatenate([dh, dl, dh], axis=0))
        for q in range(2):
            pp = pq[0:32, q * 128 : q * 128 + 128]
            qq = pq[32:64, q * 128 : q * 128 + 128]
            yy = pp - turn * pltpu.roll(qq, 64, 1)
            start = pl.multiple_of((i * 2 + q) * 8, 8)
            for j in range(4):
                gz[j, pl.ds(start, 8), :] = yy[j * 8 : j * 8 + 8, :] + ek[j, pl.ds(start, 8), :]
        return 0

    lax.fori_loop(0, 16, line, 0, unroll=16)

    dh, dl = split(jnp.concatenate([gz[j] for j in range(4)], axis=1))
    z = dot(dh, wf_h[...]) + dot(dl, wf_h[...]) + dot(dh, wf_l[...])
    for c in range(2):
        o[c] = z[:, c * 128 : c * 128 + 128]
        for b in range(8):
            out[0, c, :, b * 128 : b * 128 + 128] = o[c, pl.ds(b, 32, stride=8), :]

    rot_copy(g, 0, other).wait_send()
    pot_copy(g, 0, other).wait_send()

    def sent(i, _):
        to = mate(i)[1]
        rot_copy(g, i, to).wait_send()
        rot_copy(far, 16 + i, to).wait_send()
        pot_copy(g, i, to).wait_send()
        pot_copy(far, 16 + i, to).wait_send()
        return 0

    lax.fori_loop(1, 16, sent, 0)
    for d in range(4):
        pair_copy(d).wait_send()

        @pl.when(zl != d)
        def _():
            chip_copy(d, 0, d, 0).wait_send()
            chip_copy(d, 1, d, 0).wait_send()

    def given(i, _):
        p, to = mate(i)
        band_copy(p, 0, to).wait_send()

        @pl.when(i > 0)
        def _():
            band_copy(p, 1, to).wait_send()

        return 0

    lax.fori_loop(0, 16, given, 0)


def run(rot, pot, coef, idx, counts):
    consts = [jnp.asarray(c) for c in tables()]
    hbm = pl.BlockSpec(memory_space=pltpu.HBM)
    sems = [pltpu.SemaphoreType.DMA((n,)) for n in (14, 32, 32, 32, 32, 4, 4, 8, 10, 32, 32)]
    return pl.pallas_call(
        kernel,
        out_shape=jax.ShapeDtypeStruct((1, 2, 32, 1024), F32),
        in_specs=[hbm] * 13,
        out_specs=pl.BlockSpec(memory_space=pltpu.VMEM),
        scratch_shapes=[
            pltpu.VMEM((2, 2, 8, 128), F32),
            pltpu.VMEM((64, 128), F32),
            pltpu.VMEM((2048, 128), F32),
            pltpu.VMEM((128, 128), jnp.int32),
            pltpu.SMEM((32,), jnp.int32),
        ] + [pltpu.VMEM(c.shape, c.dtype) for c in consts] + [
            pltpu.VMEM((32, 2, 8, 256), F32),
            pltpu.VMEM((32, 64, 128), F32),
            pltpu.VMEM((512, 512), BF),
            pltpu.VMEM((512, 512), BF),
            pltpu.VMEM((4, 64, 512), F32),
            pltpu.VMEM((4, 64, 512), F32),
            pltpu.VMEM((4, 64, 512), F32),
            pltpu.VMEM((2, 5, 32, 512), F32),
            pltpu.VMEM((256, 128), F32),
            pltpu.VMEM((32, 8, 128), F32),
            pltpu.VMEM((32, 256, 512), BF),
            pltpu.VMEM((32, 128, 512), BF),
            pltpu.VMEM((512, 256), F32),
            pltpu.VMEM((4, 256, 128), F32),
            pltpu.VMEM((32 * HS, 128), F32),
            pltpu.VMEM((64 * FS, 128), F32),
            pltpu.VMEM((4, 256, 128), F32),
            pltpu.VMEM((2, 256, 128), F32),
        ] + sems + [pltpu.SemaphoreType.DMA, pltpu.SemaphoreType.DMA],
        compiler_params=pltpu.CompilerParams(
            vmem_limit_bytes=56 << 20, collective_id=0, has_side_effects=True
        ),
        name="panel",
    )(rot, pot, coef, idx, counts, *consts)


def per_device(coefficients, rotation, potential, index_map, counts):
    coef = coefficients.reshape(256, 2, 4, 128).transpose(0, 2, 1, 3).reshape(2048, 128)
    return run(
        rotation.transpose(0, 2, 1), potential, coef, index_map.reshape(128, 128), counts
    )


def solution(mesh):
    torus = Mesh(mesh.devices.reshape(4, 4, 2, 4, 2), GA + BAND)
    return jax.shard_map(
        per_device,
        mesh=torus,
        in_specs=(P(BAND, None, GA), P(None, BAND, GA), P(None, GA), P(), P()),
        out_specs=P(BAND + GA, None, None, None),
        check_vma=False,
    )
```

time: 147 us -> 56 us (0.38)
  blocking collectives: 57 us -> 0 us
  Pallas kernels: 14.1 us -> 54.2 us
  waiting for transfers between devices: 31.6 us -> 0 us
  between operations: 15.1 us -> 0.01 us
  local copies, waits for them, and re-layouts: 14.3 us -> 1.67 us
  starting transfers between devices: 12.6 us -> 0 us
  matrix products: 1.85 us -> 0 us
    all_gather x5 -> x0, blocking collectives: 57 us -> none  [gather_in_order(): parts = lax.all_gather(parts, axes[k])]
    pallas_call x1, Pallas kernels: 14.1 us -> 54.2 us  [run(): pl.pallas_call(kernel, out_shape=jax.ShapeDtypeStruct((1, 2, 32, 1024), F...]
    reduce_scatter x2 -> x0, waiting for transfers between devices: 20.3 us -> none  [the longest x1 14.5 us: sum_by_chip(): parts = lax.psum_scatter(parts, core, scatter_dimension=0, tiled=True)]
    all_to_all x1 -> x0, starting transfers between devices: 12.5 us -> none  [per_device(): vals = lax.all_to_all(summed, GA, split_axis=0, concat_axis=0, tiled=True)]
    all_gather x1 -> x0, waiting for transfers between devices: 8.3 us -> none  [gather_in_order(): parts = lax.all_gather(parts, axes[k])]
    another operation x7 -> x0, local copies, waits for them, and re-layouts: 8.18 us -> none  [the longest x4 7.69 us: mixing(): stacked = jnp.stack([upper_rows, lower_rows], axis=1)]
    all_to_all x1 -> x0, waiting for transfers between devices: 3 us -> none  [per_device(): vals = lax.all_to_all(summed, GA, split_axis=0, concat_axis=0, tiled=True)]
    transpose x3 -> x0, local copies, waits for them, and re-layouts: 2.41 us -> none  [the longest x2 1.33 us: gather_in_order(): parts = parts.transpose(*back, *range(len(axes), parts.ndim))]
  transfers between devices with their start and end apart: 4 -> 0, of which waited for: 4 -> 0; matrix products, arithmetic and copies ran while one was open for 2% -> 0% of each run, Pallas kernels for 0% -> 0%
where the time goes in v3:
time: 56 us; the launch traced here: 55.8 us
  Pallas kernels  54.2 us (97%)
  local copies, waits for them, and re-layouts  1.67 us (3%)
    pallas_call x1, Pallas kernels, run(): pl.pallas_call(kernel, out_shape=jax.ShapeDtypeStruct((1, 2, 32, 1024), F...  54.2 us
    unnamed x1, local copies, waits for them, and re-layouts  1.67 us

profile of v3, /device:TPU:32, one launch (start us, length us, event | category | flops | bytes accessed | tf_op | source)
XLA Modules:
  0.0 55.8 jit_solution(427854477235528381)
XLA Ops:
  0.0 54.2 %panel.1 = f32[1,2,32,1024]{3,2,1,0:T(8,128)} custom-call(f32[2,8,256]{2,1,0:T(8,128)} %bitcast.9, f32[64,128]{1,0:T(8,128)} %pot_in.1, f32[2048,128]{1,0:T(8,128)} %bitcast.7, s32[128,128]{1,0:T(8,128)} %bitcast.8, s32[32]{0:T(128)} %counts_in.1, bf16[256,1024]{1,0:T(8,128)(2,1)} %constant.16.clone.wz_h_in, bf16[256,1024]{1,0:T(8,128)(2,1)} %constant.17.clone.wz_l_in, ...), custom_call_target="tpu_custom_call" | custom-call | tf_op jit(solution)/shard_map/panel/pallas_call | solution.py:462
  54.2 1.7 %copy.16 = f32[1,2,32,1024]{3,2,1,0:T(8,128)} copy(f32[1,2,32,1024]{3,2,1,0:T(8,128)} %panel.1) | data formatting | bytes 524288

commit v4 on v3

--- a/solution.py
+++ b/solution.py
@@ -16,7 +16,6 @@
 BAND = ("band_0", "band_1")
 HS = 72
 FS = 40
-EARLY = 12
 
 
 def split_np(a):
@@ -180,145 +179,131 @@
         rows[k] = jnp.where(rows128 == at_row, 1.0, 0.0).astype(BF)
         return 0
 
-    lax.fori_loop(0, EARLY, one_hot, 0)
-
-    rot_copy(far, 16, other).wait_recv()
-    each(1, lambda i: rot_copy(far, 16 + i, mate(i)[1]))
-    each(1, lambda i: pot_copy(g, i, mate(i)[1]))
-    pot_copy(far, 16, other).wait_recv()
-    each(1, lambda i: pot_copy(far, 16 + i, mate(i)[1]))
-
-    lax.fori_loop(EARLY, 32, one_hot, 0)
-
     sub = lax.broadcasted_iota(jnp.int32, (8, 256), 0)
     flip = jnp.where(sub < 4, -1.0, 1.0).astype(F32)
 
-    def pair_copy(d):
-        return send(sb.at[d], sr.at[d], s_send.at[d], s_recv.at[d], sibling)
-
-    def chip_copy(d, part, to, place):
+    def row_of(n):
+        return (y + (n ^ (n >> 1))) % 4
+
+    def plane_of(q):
+        return zh if q == 0 else 1 - zh
+
+    def pair_copy(q, d):
+        return send(sb.at[q, d], sr.at[q, d], s_send.at[q * 4 + d], s_recv.at[q * 4 + d], sibling)
+
+    def chip_copy(q, d, away, src):
+        to = {"band_0": d, "ga_2": 1 - zh} if away else {"band_0": d}
         return send(
-            pb.at[d, pl.ds(part * 32, 32)], rz.at[part, place],
-            z_send.at[part * 4 + d], z_recv.at[part * 5 + place], {"band_0": to},
+            pb.at[q, d, pl.ds(away * 16, 16)], rz.at[q, away, src],
+            z_send.at[q * 8 + d * 2 + away], z_recv.at[q * 8 + src * 2 + away], to,
         )
 
-    def mix(n):
-        d = (y + (n ^ (n >> 1))) % 4
+    def mix(q, n):
+        d = row_of(n)
 
         def rot_wait(i, _):
             p, to = mate(i)
-            rot_copy(p * 2, 0, to).wait_recv()
-            rot_copy(p * 2 + 1, 0, to).wait_recv()
+            rot_copy(p * 2 + plane_of(q), 0, to).wait_recv()
             return 0
 
         lax.fori_loop(max(1, n * 4), n * 4 + 4, rot_wait, 0)
         left, right = [], []
         for parity in (1 - core, core):
-            for s in (1 - zh, zh):
-                for k in range(4):
-                    block = rg[d * 8 + parity * 4 + k, s]
+            for t in (zh, 1 - zh):
+                for xb in range(2):
+                    block = rg[d * 8 + (parity * 2 + xb) * 2 + plane_of(q), t]
                     left.append(block)
                     right.append(flip * pltpu.roll(block, 4, 0))
         lh, ll = split(jnp.concatenate([jnp.concatenate(left, 0), jnp.concatenate(right, 0)], 1))
-        both = dot(lh, ch[...]) + dot(ll, ch[...]) + dot(lh, cl[...])
-        sb[d] = both[0:64]
-        pb[d] = both[64:128]
-        pair_copy(d).start()
-
-    def scatter_half(n, part):
-        d = (y + (n ^ (n >> 1))) % 4
-        up = (zl == 0) & (d == 2)
-        down = (zl == 3) & (d == 1)
-        wait_for = ((zl == 1) & (d == 2)) | ((zl == 2) & (d == 1))
-
-        @pl.when((d != zl) & jnp.logical_not(wait_for))
+        high = dot(jnp.concatenate([lh, ll], axis=0), ch[...])
+        both = high[0:64] + high[64:128] + dot(lh, cl[...])
+        sb[q, d] = both[0:32]
+        pb[q, d] = both[32:64]
+        pair_copy(q, d).start()
+
+    def settle(q, n):
+        d = row_of(n)
+        pair_copy(q, d).wait_recv()
+        pb[q, d] = pb[q, d] + sr[q, d]
+        chip_copy(q, d, 1, zl).start()
+
+        @pl.when(d != zl)
         def _():
-            to = jnp.where(up, 1, jnp.where(down, 2, d))
-            place = jnp.where(up | down, 4, zl)
-            chip_copy(d, part, to, place).start()
-
-    def settle(n):
-        d = (y + (n ^ (n >> 1))) % 4
-        pair_copy(d).wait_recv()
-        pb[d] = pb[d] + sr[d]
-        scatter_half(n, 0)
-
-    mix(0)
-    for n in range(1, 4):
-        mix(n)
-        settle(n - 1)
-    settle(3)
-
-    def merge(part):
-        @pl.when((zl == 1) | (zl == 2))
-        def _():
-            d = 3 - zl
-            chip_copy(d, part, d, 4).wait_recv()
-            pb[d, part * 32 : part * 32 + 32] = pb[d, part * 32 : part * 32 + 32] + rz[part, 4]
-            chip_copy(d, part, d, zl).start()
-
-    def band_copy(p, part, to):
-        s = (1 - zh) if part == 0 else zh
-        gg = p * 2 + s
-        src = ab.at[pl.ds(pl.multiple_of(gg * 8, 8), 8)]
-        return send(src, vals.at[g], a_send.at[gg], a_recv.at[g], {**to, "ga_2": s})
-
-    def finish(part):
-        s = (1 - zh) if part == 0 else zh
-        for src in range(4):
-            skip = (zl == src) | ((zl == 2) & (src == 0)) | ((zl == 1) & (src == 3))
-
-            @pl.when(jnp.logical_not(skip))
+            chip_copy(q, d, 0, zl).start()
+
+    def band_copy(q, i):
+        away, xb, xx = 1 - i // 8, (i // 4) % 2, (x + 3 - i % 4) % 4
+        source = plane_of(away)
+        yy = xb * 2 + plane_of(q ^ away)
+        slot16 = yy * 4 + xx
+        src = ab.at[pl.ds(pl.multiple_of(away * 128 + slot16 * 8, 8), 8)]
+        block = (y * 4 + x) * 2 + source
+        to = {"ga_0": yy, "ga_1": xx}
+        return slot16, send(
+            src, vals.at[block], a_send.at[away * 16 + slot16], a_recv.at[block], to
+        )
+
+    def finish(q):
+        for away in (1, 0):
+            total = pb[q, zl, 0:16, :] if away == 0 else None
+            for i in range(1 - away, 4):
+                src = (zl + i) % 4
+                chip_copy(q, zl, away, src).wait_recv()
+                part = rz[q, away, src]
+                total = part if total is None else total + part
+            for xb in range(2):
+                for c in range(2):
+                    for t in range(4):
+                        start = away * 128 + (xb * 2 + plane_of(q ^ away)) * 32 + c * 4 + t
+                        at = xb * 8 + c * 4
+                        ab[pl.ds(start, 4, stride=8), :] = total[at : at + 4, t * 128 : t * 128 + 128]
+            for i in range(8):
+                slot16, copy = band_copy(q, i + 8 * (1 - away))
+
+                @pl.when(slot16 != y * 4 + x)
+                def _():
+                    copy.start()
+
+    lax.fori_loop(0, 32, one_hot, 0)
+    mix(0, 0)
+    rot_copy(far, 16, other).wait_recv()
+    each(1, lambda i: rot_copy(far, 16 + i, mate(i)[1]))
+    settle(0, 0)
+    mix(0, 1)
+    mix(0, 2)
+    settle(0, 1)
+    each(1, lambda i: pot_copy(g, i, mate(i)[1]))
+    mix(0, 3)
+    settle(0, 2)
+    mix(1, 0)
+    settle(0, 3)
+    mix(1, 1)
+    settle(1, 0)
+    mix(1, 2)
+    settle(1, 1)
+    mix(1, 3)
+    settle(1, 2)
+    settle(1, 3)
+    pot_copy(far, 16, other).wait_recv()
+    each(1, lambda i: pot_copy(far, 16 + i, mate(i)[1]))
+    finish(0)
+    finish(1)
+    home = pl.multiple_of((y * 4 + x) * 8, 8)
+    vals[g] = ab[pl.ds(home, 8), :]
+    vals[far] = ab[pl.ds(home + 128, 8), :]
+
+    def place(i, plane):
+        left, right = [], []
+        for b in range(4):
+            p, to = mate(i * 4 + b)
+            k = p * 2 + plane
+
+            @pl.when(p != y * 4 + x)
             def _():
-                chip_copy(zl, part, zl, src).wait_recv()
-                pb[zl, part * 32 : part * 32 + 32] = (
-                    pb[zl, part * 32 : part * 32 + 32] + rz[part, src]
-                )
-
-        total = pb[zl, part * 32 : part * 32 + 32]
-        for k in range(4):
-            for c in range(2):
-                for t in range(4):
-                    piece = total[k * 8 + c * 4 : k * 8 + c * 4 + 4, t * 128 : t * 128 + 128]
-                    ab[pl.ds(k * 64 + s * 8 + c * 4 + t, 4, stride=16), :] = piece
-
-        def out_step(i, _):
-            p, to = mate(15 - i)
-            band_copy(p, part, to).start()
-            return 0
-
-        lax.fori_loop(0, 16 - part, out_step, 0)
-
-    merge(0)
-    for n in range(4):
-        scatter_half(n, 1)
-    finish(0)
-    merge(1)
-    finish(1)
-    vals[g] = ab[pl.ds(pl.multiple_of(g * 8, 8), 8), :]
-
-    def pot_wait(i, _):
-        p, to = mate(i)
-        pot_copy(p * 2, 0, to).wait_recv()
-        pot_copy(p * 2 + 1, 0, to).wait_recv()
-        return 0
-
-    lax.fori_loop(1, 16, pot_wait, 0)
-    side = vg.at[:, pl.ds(half, 32)]
-    swap = send(side, side, w_send, w_recv, sibling)
-    swap.start()
-
-    def place(i, first=False):
-        p, to = mate(i)
-        if first:
-            send(ab.at[pl.ds(0, 8)], vals.at[far], a_send.at[0], a_recv.at[far], to).wait_recv()
-        else:
-            for q in range(2):
-                k = p * 2 + q
                 send(ab.at[pl.ds(0, 8)], vals.at[k], a_send.at[0], a_recv.at[k], to).wait_recv()
-        left = []
-        for q in range(2):
-            k = p * 2 + q
+
+        for b in range(4):
+            k = mate(i * 4 + b)[0] * 2 + plane
             hit = rows[k]
             parts = []
             for c in range(2):
@@ -328,23 +313,36 @@
                     wide = jnp.broadcast_to(part, (16, 512)).astype(BF)
                     parts.append(hit * jnp.concatenate([wide] * 8, axis=0))
             left.append(jnp.concatenate(parts, axis=0))
-        right = jnp.concatenate([cols[p * 2], cols[p * 2 + 1]], axis=1)
-        placed = lax.dot_general(
-            jnp.concatenate(left, axis=1), right, (((1,), (1,)), ((), ())),
-            preferred_element_type=F32,
+            right.append(cols[k])
+        return lax.dot_general(
+            jnp.concatenate(left, axis=1), jnp.concatenate(right, axis=1),
+            (((1,), (1,)), ((), ())), preferred_element_type=F32,
         )
-        if first:
-            acc[...] = placed
-        else:
-            acc[...] += placed
-
-    place(0, True)
-
-    def place_step(i, _):
-        place(i)
-        return 0
-
-    lax.fori_loop(1, 16, place_step, 0)
+
+    soon = y % 2
+    acc[...] = place(0, soon)
+
+    def place_soon(i, _):
+        acc[...] += place(i, soon)
+        return 0
+
+    def place_late(i, _):
+        acc[...] += place(i, 1 - soon)
+        return 0
+
+    lax.fori_loop(1, 4, place_soon, 0)
+
+    def pot_wait(i, _):
+        p, to = mate(i)
+        pot_copy(p * 2, 0, to).wait_recv()
+        pot_copy(p * 2 + 1, 0, to).wait_recv()
+        return 0
+
+    lax.fori_loop(1, 16, pot_wait, 0)
+    side = vg.at[:, pl.ds(half, 32)]
+    swap = send(side, side, w_send, w_recv, sibling)
+    swap.start()
+    lax.fori_loop(0, 4, place_late, 0)
 
     for copy in local[5:13]:
         copy.wait()
@@ -434,31 +432,27 @@
         return 0
 
     lax.fori_loop(1, 16, sent, 0)
-    for d in range(4):
-        pair_copy(d).wait_send()
-
-        @pl.when(zl != d)
-        def _():
-            chip_copy(d, 0, d, 0).wait_send()
-            chip_copy(d, 1, d, 0).wait_send()
-
-    def given(i, _):
-        p, to = mate(i)
-        band_copy(p, 0, to).wait_send()
-
-        @pl.when(i > 0)
-        def _():
-            band_copy(p, 1, to).wait_send()
-
-        return 0
-
-    lax.fori_loop(0, 16, given, 0)
+    for q in range(2):
+        for d in range(4):
+            pair_copy(q, d).wait_send()
+            chip_copy(q, d, 1, 0).wait_send()
+
+            @pl.when(zl != d)
+            def _():
+                chip_copy(q, d, 0, 0).wait_send()
+
+        for i in range(16):
+            slot16, copy = band_copy(q, i)
+
+            @pl.when(slot16 != y * 4 + x)
+            def _():
+                copy.wait_send()
 
 
 def run(rot, pot, coef, idx, counts):
     consts = [jnp.asarray(c) for c in tables()]
     hbm = pl.BlockSpec(memory_space=pltpu.HBM)
-    sems = [pltpu.SemaphoreType.DMA((n,)) for n in (14, 32, 32, 32, 32, 4, 4, 8, 10, 32, 32)]
+    sems = [pltpu.SemaphoreType.DMA((n,)) for n in (14, 32, 32, 32, 32, 8, 8, 16, 16, 32, 32)]
     return pl.pallas_call(
         kernel,
         out_shape=jax.ShapeDtypeStruct((1, 2, 32, 1024), F32),
@@ -475,10 +469,10 @@
             pltpu.VMEM((32, 64, 128), F32),
             pltpu.VMEM((512, 512), BF),
             pltpu.VMEM((512, 512), BF),
-            pltpu.VMEM((4, 64, 512), F32),
-            pltpu.VMEM((4, 64, 512), F32),
-            pltpu.VMEM((4, 64, 512), F32),
-            pltpu.VMEM((2, 5, 32, 512), F32),
+            pltpu.VMEM((2, 4, 32, 512), F32),
+            pltpu.VMEM((2, 4, 32, 512), F32),
+            pltpu.VMEM((2, 4, 32, 512), F32),
+            pltpu.VMEM((2, 2, 4, 16, 512), F32),
             pltpu.VMEM((256, 128), F32),
             pltpu.VMEM((32, 8, 128), F32),
             pltpu.VMEM((32, 256, 512), BF),

time: 56 us -> 45.8 us (0.82); the launches traced: 55.8 us -> 45 us
  Pallas kernels: 54.2 us -> 43.3 us
    pallas_call x1, Pallas kernels: 54.2 us -> 43.3 us  [run(): pl.pallas_call(kernel, out_shape=jax.ShapeDtypeStruct((1, 2, 32, 1024), F...]
where the time goes in v4:
time: 45.8 us; the launch traced here: 45 us
  Pallas kernels  43.3 us (95%)
  local copies, waits for them, and re-layouts  1.67 us (4%)
    pallas_call x1, Pallas kernels, run(): pl.pallas_call(kernel, out_shape=jax.ShapeDtypeStruct((1, 2, 32, 1024), F...  43.3 us
    unnamed x1, local copies, waits for them, and re-layouts  1.67 us

profile of v4, /device:TPU:32, one launch (start us, length us, event | category | flops | bytes accessed | tf_op | source)
XLA Modules:
  0.0 45.0 jit_solution(1781239632451547707)
XLA Ops:
  0.0 43.3 %panel.1 = f32[1,2,32,1024]{3,2,1,0:T(8,128)} custom-call(f32[2,8,256]{2,1,0:T(8,128)} %bitcast.9, f32[64,128]{1,0:T(8,128)} %pot_in.1, f32[2048,128]{1,0:T(8,128)} %bitcast.7, s32[128,128]{1,0:T(8,128)} %bitcast.8, s32[32]{0:T(128)} %counts_in.1, bf16[256,1024]{1,0:T(8,128)(2,1)} %constant.16.clone.wz_h_in, bf16[256,1024]{1,0:T(8,128)(2,1)} %constant.17.clone.wz_l_in, ...), custom_call_target="tpu_custom_call" | custom-call | tf_op jit(solution)/shard_map/panel/pallas_call | solution.py:456
  43.3 1.7 %copy.16 = f32[1,2,32,1024]{3,2,1,0:T(8,128)} copy(f32[1,2,32,1024]{3,2,1,0:T(8,128)} %panel.1) | data formatting | bytes 524288

commit v5 on v4

--- a/solution.py
+++ b/solution.py
@@ -94,8 +94,8 @@
             (rot_in.at[:, :, 128:256], rot.at[1]),
         ])
     ]
-    for n in (0, 13, *range(1, 13)):
-        local[n].start()
+    local[0].start()
+    local[13].start()
 
     def mate(i):
         a, b = i // 4, i % 4
@@ -106,18 +106,21 @@
     barrier = pltpu.get_barrier_semaphore()
 
     def greet(i, _):
-        pl.semaphore_signal(barrier, inc=1, device_id=mate(i)[1], device_id_type=MESH)
+        pl.semaphore_signal(barrier, inc=1, device_id=mate(16 - i)[1], device_id_type=MESH)
         return 0
 
     def hop(i, _):
-        pl.semaphore_signal(barrier, inc=1, device_id={"band_0": (zl + i) % 4}, device_id_type=MESH)
+        p = (zl * 2 + core + i) % 8
+        to = {"band_0": p // 2, "band_1": p % 2}
+        pl.semaphore_signal(barrier, inc=1, device_id=to, device_id_type=MESH)
         return 0
 
     pl.semaphore_signal(barrier, inc=1, device_id=other, device_id_type=MESH)
     lax.fori_loop(1, 16, greet, 0)
-    lax.fori_loop(1, 4, hop, 0)
-    pl.semaphore_signal(barrier, inc=1, device_id=sibling, device_id_type=MESH)
-
+    lax.fori_loop(1, 8, hop, 0)
+
+    for n in range(1, 13):
+        local[n].start()
     local[0].wait()
     local[13].wait()
     for t in range(2):
@@ -128,7 +131,7 @@
                 ]
     local[2].wait()
     vg[g, pl.ds(half, 32), :] = pot[pl.ds(half, 32), :]
-    pl.semaphore_wait(barrier, 20)
+    pl.semaphore_wait(barrier, 23)
 
     def send(src, dst, send_sem, recv_sem, to):
         return pltpu.make_async_remote_copy(
@@ -143,12 +146,12 @@
         piece = vg.at[block, pl.ds(half, 32)]
         return send(piece, piece, v_send.at[i], v_recv.at[block], to)
 
-    def each(lo, copy):
+    def each(lo, copy, hi=16):
         def step(i, _):
             copy(i).start()
             return 0
 
-        lax.fori_loop(lo, 16, step, 0)
+        lax.fori_loop(lo, hi, step, 0)
 
     rot_copy(g, 0, other).start()
     each(1, lambda i: rot_copy(g, i, mate(i)[1]))
@@ -179,6 +182,7 @@
         rows[k] = jnp.where(rows128 == at_row, 1.0, 0.0).astype(BF)
         return 0
 
+    acc[...] = jnp.zeros_like(acc)
     sub = lax.broadcasted_iota(jnp.int32, (8, 256), 0)
     flip = jnp.where(sub < 4, -1.0, 1.0).astype(F32)
 
@@ -192,7 +196,9 @@
         return send(sb.at[q, d], sr.at[q, d], s_send.at[q * 4 + d], s_recv.at[q * 4 + d], sibling)
 
     def chip_copy(q, d, away, src):
-        to = {"band_0": d, "ga_2": 1 - zh} if away else {"band_0": d}
+        to = {"band_0": d, **sibling}
+        if away:
+            to["ga_2"] = 1 - zh
         return send(
             pb.at[q, d, pl.ds(away * 16, 16)], rz.at[q, away, src],
             z_send.at[q * 8 + d * 2 + away], z_recv.at[q * 8 + src * 2 + away], to,
@@ -226,10 +232,7 @@
         pair_copy(q, d).wait_recv()
         pb[q, d] = pb[q, d] + sr[q, d]
         chip_copy(q, d, 1, zl).start()
-
-        @pl.when(d != zl)
-        def _():
-            chip_copy(q, d, 0, zl).start()
+        chip_copy(q, d, 0, zl).start()
 
     def band_copy(q, i):
         away, xb, xx = 1 - i // 8, (i // 4) % 2, (x + 3 - i % 4) % 4
@@ -238,16 +241,15 @@
         slot16 = yy * 4 + xx
         src = ab.at[pl.ds(pl.multiple_of(away * 128 + slot16 * 8, 8), 8)]
         block = (y * 4 + x) * 2 + source
-        to = {"ga_0": yy, "ga_1": xx}
-        return slot16, send(
+        to = {"ga_0": yy, "ga_1": xx, **sibling}
+        return send(
             src, vals.at[block], a_send.at[away * 16 + slot16], a_recv.at[block], to
         )
 
     def finish(q):
         for away in (1, 0):
-            total = pb[q, zl, 0:16, :] if away == 0 else None
-            for i in range(1 - away, 4):
-                src = (zl + i) % 4
+            total = None
+            for src in range(4):
                 chip_copy(q, zl, away, src).wait_recv()
                 part = rz[q, away, src]
                 total = part if total is None else total + part
@@ -258,49 +260,47 @@
                         at = xb * 8 + c * 4
                         ab[pl.ds(start, 4, stride=8), :] = total[at : at + 4, t * 128 : t * 128 + 128]
             for i in range(8):
-                slot16, copy = band_copy(q, i + 8 * (1 - away))
-
-                @pl.when(slot16 != y * 4 + x)
-                def _():
-                    copy.start()
+                band_copy(q, i + 8 * (1 - away)).start()
 
     lax.fori_loop(0, 32, one_hot, 0)
     mix(0, 0)
     rot_copy(far, 16, other).wait_recv()
     each(1, lambda i: rot_copy(far, 16 + i, mate(i)[1]))
+    mix(0, 1)
     settle(0, 0)
-    mix(0, 1)
     mix(0, 2)
     settle(0, 1)
-    each(1, lambda i: pot_copy(g, i, mate(i)[1]))
     mix(0, 3)
     settle(0, 2)
     mix(1, 0)
     settle(0, 3)
+    each(1, lambda i: pot_copy(g, i, mate(i)[1]))
     mix(1, 1)
     settle(1, 0)
+    pot_copy(far, 16, other).wait_recv()
+    each(1, lambda i: pot_copy(far, 16 + i, mate(i)[1]))
     mix(1, 2)
     settle(1, 1)
     mix(1, 3)
     settle(1, 2)
     settle(1, 3)
-    pot_copy(far, 16, other).wait_recv()
-    each(1, lambda i: pot_copy(far, 16 + i, mate(i)[1]))
     finish(0)
+    def pot_wait(i, _):
+        p, to = mate(i)
+        pot_copy(p * 2, 0, to).wait_recv()
+        pot_copy(p * 2 + 1, 0, to).wait_recv()
+        return 0
+
+    lax.fori_loop(1, 16, pot_wait, 0)
+    side = vg.at[:, pl.ds(half, 32)]
+    swap = send(side, side, w_send, w_recv, sibling)
+    swap.start()
     finish(1)
-    home = pl.multiple_of((y * 4 + x) * 8, 8)
-    vals[g] = ab[pl.ds(home, 8), :]
-    vals[far] = ab[pl.ds(home + 128, 8), :]
-
     def place(i, plane):
         left, right = [], []
         for b in range(4):
-            p, to = mate(i * 4 + b)
-            k = p * 2 + plane
-
-            @pl.when(p != y * 4 + x)
-            def _():
-                send(ab.at[pl.ds(0, 8)], vals.at[k], a_send.at[0], a_recv.at[k], to).wait_recv()
+            k = mate(i * 4 + b)[0] * 2 + plane
+            send(ab.at[pl.ds(0, 8)], vals.at[k], a_send.at[0], a_recv.at[k], sibling).wait_recv()
 
         for b in range(4):
             k = mate(i * 4 + b)[0] * 2 + plane
@@ -320,29 +320,11 @@
         )
 
     soon = y % 2
-    acc[...] = place(0, soon)
-
-    def place_soon(i, _):
-        acc[...] += place(i, soon)
-        return 0
-
-    def place_late(i, _):
-        acc[...] += place(i, 1 - soon)
-        return 0
-
-    lax.fori_loop(1, 4, place_soon, 0)
-
-    def pot_wait(i, _):
-        p, to = mate(i)
-        pot_copy(p * 2, 0, to).wait_recv()
-        pot_copy(p * 2 + 1, 0, to).wait_recv()
-        return 0
-
-    lax.fori_loop(1, 16, pot_wait, 0)
-    side = vg.at[:, pl.ds(half, 32)]
-    swap = send(side, side, w_send, w_recv, sibling)
-    swap.start()
-    lax.fori_loop(0, 4, place_late, 0)
+    def place_step(i, _):
+        acc[...] += place(i % 4, jnp.where(i < 4, soon, 1 - soon))
+        return 0
+
+    lax.fori_loop(0, 8, place_step, 0)
 
     for copy in local[5:13]:
         copy.wait()
@@ -396,7 +378,7 @@
             f[pl.ds(start, 32), :] = pp - turn * pltpu.roll(qq, 64, 1)
         return 0
 
-    lax.fori_loop(0, 32, plane, 0, unroll=16)
+    lax.fori_loop(0, 32, plane, 0, unroll=32)
 
     def line(i, _):
         d = jnp.concatenate([f[pl.ds(i * 2 + q, 64, stride=FS), :] for q in range(2)], axis=1)
@@ -436,17 +418,9 @@
         for d in range(4):
             pair_copy(q, d).wait_send()
             chip_copy(q, d, 1, 0).wait_send()
-
-            @pl.when(zl != d)
-            def _():
-                chip_copy(q, d, 0, 0).wait_send()
-
+            chip_copy(q, d, 0, 0).wait_send()
         for i in range(16):
-            slot16, copy = band_copy(q, i)
-
-            @pl.when(slot16 != y * 4 + x)
-            def _():
-                copy.wait_send()
+            band_copy(q, i).wait_send()
 
 
 def run(rot, pot, coef, idx, counts):

time: 45.8 us -> 44.7 us (0.976)
  the two profiles are of different devices: /device:TPU:32 before, /device:TPU:1 now
where the time goes in v5:
time: 44.7 us; the launch traced here: 44.5 us
  Pallas kernels  42.8 us (96%)
  local copies, waits for them, and re-layouts  1.67 us (4%)
    pallas_call x1, Pallas kernels, run(): pl.pallas_call(kernel, out_shape=jax.ShapeDtypeStruct((1, 2, 32, 1024), F...  42.8 us
    unnamed x1, local copies, waits for them, and re-layouts  1.67 us

profile of v5, /device:TPU:1, one launch (start us, length us, event | category | flops | bytes accessed | tf_op | source)
XLA Modules:
  0.0 44.5 jit_solution(17925323491260991680)
XLA Ops:
  0.0 42.8 %panel.1 = f32[1,2,32,1024]{3,2,1,0:T(8,128)} custom-call(f32[2,8,256]{2,1,0:T(8,128)} %bitcast.9, f32[64,128]{1,0:T(8,128)} %pot_in.1, f32[2048,128]{1,0:T(8,128)} %bitcast.7, s32[128,128]{1,0:T(8,128)} %bitcast.8, s32[32]{0:T(128)} %counts_in.1, bf16[256,1024]{1,0:T(8,128)(2,1)} %constant.16.clone.wz_h_in, bf16[256,1024]{1,0:T(8,128)(2,1)} %constant.17.clone.wz_l_in, ...), custom_call_target="tpu_custom_call" | custom-call | tf_op jit(solution)/shard_map/panel/pallas_call | solution.py:430
  42.9 1.7 %copy.16 = f32[1,2,32,1024]{3,2,1,0:T(8,128)} copy(f32[1,2,32,1024]{3,2,1,0:T(8,128)} %panel.1) | data formatting | bytes 524288

commit v6 on v5

--- a/solution.py
+++ b/solution.py
@@ -36,15 +36,13 @@
     ang = 2.0 * math.pi * ((r[:, None] * n[None, :]) % 64) / 64.0
     cos, sin = np.cos(ang), np.sin(ang)
     perm = np.array([(k % 8) * 4 + k // 8 for k in range(32)])
-    s = 8.0 / 4096.0
-    wz = np.zeros((2, 4, 32, 2, 4, 2, 64))
+    wz = np.zeros((2, 4, 32, 4, 2, 64))
     for q in range(4):
-        wz[0, q, :, 0, q, 0, :] = cos.T / 64
-        wz[1, q, :, 0, q, 0, :] = -sin.T / 64
-        wz[0, q, :, 0, q, 1, :] = sin.T / 64
-        wz[1, q, :, 0, q, 1, :] = cos.T / 64
-    wz[:, :, :, 1] = wz[:, :, :, 0] * (s * n * n)[None, None, :, None, None, None]
-    wz_h, wz_l = split_np(wz.reshape(256, 1024))
+        wz[0, q, :, q, 0, :] = cos.T / 64
+        wz[1, q, :, q, 0, :] = -sin.T / 64
+        wz[0, q, :, q, 1, :] = sin.T / 64
+        wz[1, q, :, q, 1, :] = cos.T / 64
+    wz_h, wz_l = split_np(wz.reshape(256, 512))
     ty = stack3(np.concatenate([cos[:, perm], sin[:, perm]], axis=1) / 64)
     tx = stack3(np.concatenate([cos, sin], axis=1) / 64)
     fx = stack3(np.concatenate([cos.T, sin.T], axis=0))
@@ -73,7 +71,7 @@
     wz_h_in, wz_l_in, ty_in, tx_in, fx_in, fy_in, wf_h_in, wf_l_in,
     out,
     rot, pot, coef, idx, counts, wz_h, wz_l, ty, tx, fx, fy, wf_h, wf_l,
-    rg, vg, ch, cl, sb, sr, pb, rz, ab, vals, cols, rows, acc, ek, h, f, gz, o,
+    rg, vg, ch, cl, sb, sr, pb, rz, ab, vals, cols, rows, acc, ek, h, f, gz, o, res,
     l_sem, r_send, r_recv, v_send, v_recv, s_send, s_recv, z_send, z_recv,
     a_send, a_recv, w_send, w_recv,
 ):
@@ -332,22 +330,54 @@
     turn = jnp.where(lane < 64, -1.0, 1.0).astype(F32)
     re = acc[0:128, :] + acc[128:256, :]
     im = acc[256:384, :] + acc[384:512, :]
-    nrow = lax.broadcasted_iota(jnp.int32, (32, 128), 0)
-    ny = ((nrow & 7) * 4 + (nrow >> 3) - 16).astype(F32)
-    ksq = (8.0 / 4096.0) * ny * ny
-    e = []
-    for t in range(2):
-        d = jnp.concatenate([re[:, t * 128 : t * 128 + 128], im[:, t * 128 : t * 128 + 128]], axis=1)
-        dh, dl = split(d)
-        e.append(dot(dh, wz_h[...]) + dot(dl, wz_h[...]) + dot(dh, wz_l[...]))
+    both = jnp.concatenate([re, im], axis=1)
+    d = jnp.concatenate(
+        [
+            jnp.concatenate([v[:, t * 128 : t * 128 + 128] for v in (re, im)], axis=1)
+            for t in range(2)
+        ],
+        axis=0,
+    )
+    dh, dl = split(d)
+    e = dot(dh, wz_h[...]) + dot(dl, wz_h[...]) + dot(dh, wz_l[...])
+
+    lane8 = lax.broadcasted_iota(jnp.int32, (8, 128), 1)
+    high = lax.broadcasted_iota(jnp.int32, (8, 128), 0)
+    ny = (high * 4 + (lane8 >> 5) - 16).astype(F32)
+    nz = ((lane8 & 31) - 16).astype(F32)
+    kyz = (8.0 / 4096.0) * (ny * ny + nz * nz)
+    quarter = lax.broadcasted_iota(jnp.int32, (1, 128), 1) >> 5
+    lines = [
+        jnp.concatenate(
+            [
+                both[xh * 32 + j * 8 : xh * 32 + j * 8 + 8, ct * 128 : ct * 128 + 128]
+                for ct in range(4)
+                for xh in range(4)
+            ],
+            axis=0,
+        )
+        for j in range(4)
+    ]
+    for q in range(4):
+        turned = [
+            lines[j] if j == q else pltpu.roll(lines[j], ((j - q) * 32) % 128, 1) for j in range(4)
+        ]
+        mixed = jnp.where(
+            quarter < 2,
+            jnp.where(quarter == 0, turned[0], turned[1]),
+            jnp.where(quarter == 2, turned[2], turned[3]),
+        )
+        for ct in range(4):
+            for xh in range(4):
+                i = xh * 8 + (ct % 2) * 4 + q
+                kin = kyz + (8.0 / 4096.0) * (i - 16) ** 2
+                at = (ct * 4 + xh) * 8
+                ek[ct // 2, i * 8 : i * 8 + 8, :] = kin * mixed[at : at + 8, :]
 
     def column(i):
         xh, t, q = i // 8, (i // 4) % 2, i % 4
-        tile = e[t][xh * 32 : xh * 32 + 32, q * 128 : q * 128 + 128]
-        bent = e[t][xh * 32 : xh * 32 + 32, 512 + q * 128 : 512 + q * 128 + 128]
-        kin = (ksq + (8.0 / 4096.0) * (i - 16) ** 2) * tile + bent
-        for j in range(4):
-            ek[j, i * 8 : i * 8 + 8, :] = kin[j * 8 : j * 8 + 8, :]
+        at = t * 128 + xh * 32
+        tile = e[at : at + 32, q * 128 : q * 128 + 128]
         return jnp.concatenate([tile, turn * pltpu.roll(tile, 64, 1)], axis=0)
 
     for i in range(0, 32, 2):
@@ -390,17 +420,21 @@
             yy = pp - turn * pltpu.roll(qq, 64, 1)
             start = pl.multiple_of((i * 2 + q) * 8, 8)
             for j in range(4):
-                gz[j, pl.ds(start, 8), :] = yy[j * 8 : j * 8 + 8, :] + ek[j, pl.ds(start, 8), :]
+                gz[j, pl.ds(start, 8), :] = yy[j * 8 : j * 8 + 8, :]
         return 0
 
     lax.fori_loop(0, 16, line, 0, unroll=16)
 
     dh, dl = split(jnp.concatenate([gz[j] for j in range(4)], axis=1))
     z = dot(dh, wf_h[...]) + dot(dl, wf_h[...]) + dot(dh, wf_l[...])
+    def result(c):
+        return pltpu.make_async_copy(res.at[c], out.at[0, c], l_sem.at[c])
+
     for c in range(2):
-        o[c] = z[:, c * 128 : c * 128 + 128]
+        o[c] = z[:, c * 128 : c * 128 + 128] + ek[c]
         for b in range(8):
-            out[0, c, :, b * 128 : b * 128 + 128] = o[c, pl.ds(b, 32, stride=8), :]
+            res[c, :, b * 128 : b * 128 + 128] = o[c, pl.ds(b, 32, stride=8), :]
+        result(c).start()
 
     rot_copy(g, 0, other).wait_send()
     pot_copy(g, 0, other).wait_send()
@@ -421,6 +455,8 @@
             chip_copy(q, d, 0, 0).wait_send()
         for i in range(16):
             band_copy(q, i).wait_send()
+    for c in range(2):
+        result(c).wait()
 
 
 def run(rot, pot, coef, idx, counts):
@@ -431,7 +467,7 @@
         kernel,
         out_shape=jax.ShapeDtypeStruct((1, 2, 32, 1024), F32),
         in_specs=[hbm] * 13,
-        out_specs=pl.BlockSpec(memory_space=pltpu.VMEM),
+        out_specs=hbm,
         scratch_shapes=[
             pltpu.VMEM((2, 2, 8, 128), F32),
             pltpu.VMEM((64, 128), F32),
@@ -452,11 +488,12 @@
             pltpu.VMEM((32, 256, 512), BF),
             pltpu.VMEM((32, 128, 512), BF),
             pltpu.VMEM((512, 256), F32),
-            pltpu.VMEM((4, 256, 128), F32),
+            pltpu.VMEM((2, 256, 128), F32),
             pltpu.VMEM((32 * HS, 128), F32),
             pltpu.VMEM((64 * FS, 128), F32),
             pltpu.VMEM((4, 256, 128), F32),
             pltpu.VMEM((2, 256, 128), F32),
+            pltpu.VMEM((2, 32, 1024), F32),
         ] + sems + [pltpu.SemaphoreType.DMA, pltpu.SemaphoreType.DMA],
         compiler_params=pltpu.CompilerParams(
             vmem_limit_bytes=56 << 20, collective_id=0, has_side_effects=True

time: 44.7 us -> 44.5 us (level)
  no operation moved by 1% of the time
where the time goes in v6:
time: 44.5 us; the launch traced here: 44.3 us
  Pallas kernels  42.6 us (96%)
  local copies, waits for them, and re-layouts  1.67 us (4%)
    pallas_call x1, Pallas kernels, run(): pl.pallas_call(kernel, out_shape=jax.ShapeDtypeStruct((1, 2, 32, 1024), F...  42.6 us
    unnamed x1, local copies, waits for them, and re-layouts  1.67 us

profile of v6, /device:TPU:1, one launch (start us, length us, event | category | flops | bytes accessed | tf_op | source)
XLA Modules:
  0.0 44.3 jit_solution(8615453601865103395)
XLA Ops:
  0.0 42.6 %panel.1 = f32[1,2,32,1024]{3,2,1,0:T(8,128)} custom-call(f32[2,8,256]{2,1,0:T(8,128)} %bitcast.9, f32[64,128]{1,0:T(8,128)} %pot_in.1, f32[2048,128]{1,0:T(8,128)} %bitcast.7, s32[128,128]{1,0:T(8,128)} %bitcast.8, s32[32]{0:T(128)} %counts_in.1, bf16[256,512]{1,0:T(8,128)(2,1)} %constant.16.clone.wz_h_in, bf16[256,512]{1,0:T(8,128)(2,1)} %constant.17.clone.wz_l_in, ...), custom_call_target="tpu_custom_call" | custom-call | tf_op jit(solution)/shard_map/panel/pallas_call | solution.py:466
  42.7 1.7 %copy.16 = f32[1,2,32,1024]{3,2,1,0:T(8,128)} copy(f32[1,2,32,1024]{3,2,1,0:T(8,128)} %panel.1) | data formatting | bytes 524288

commit v7 on v6

--- a/solution.py
+++ b/solution.py
@@ -229,8 +229,8 @@
         d = row_of(n)
         pair_copy(q, d).wait_recv()
         pb[q, d] = pb[q, d] + sr[q, d]
+        chip_copy(q, d, 0, zl).start()
         chip_copy(q, d, 1, zl).start()
-        chip_copy(q, d, 0, zl).start()
 
     def band_copy(q, i):
         away, xb, xx = 1 - i // 8, (i // 4) % 2, (x + 3 - i % 4) % 4
@@ -272,16 +272,16 @@
     settle(0, 2)
     mix(1, 0)
     settle(0, 3)
-    each(1, lambda i: pot_copy(g, i, mate(i)[1]))
     mix(1, 1)
     settle(1, 0)
-    pot_copy(far, 16, other).wait_recv()
-    each(1, lambda i: pot_copy(far, 16 + i, mate(i)[1]))
+    each(1, lambda i: pot_copy(g, i, mate(i)[1]))
     mix(1, 2)
     settle(1, 1)
     mix(1, 3)
     settle(1, 2)
     settle(1, 3)
+    pot_copy(far, 16, other).wait_recv()
+    each(1, lambda i: pot_copy(far, 16 + i, mate(i)[1]))
     finish(0)
     def pot_wait(i, _):
         p, to = mate(i)

time: 44.5 us -> 44.5 us (level)
  no operation moved by 1% of the time
where the time goes in v7:
time: 44.5 us; the launch traced here: 44.4 us
  Pallas kernels  42.7 us (96%)
  local copies, waits for them, and re-layouts  1.67 us (4%)
    pallas_call x1, Pallas kernels, run(): pl.pallas_call(kernel, out_shape=jax.ShapeDtypeStruct((1, 2, 32, 1024), F...  42.7 us
    unnamed x1, local copies, waits for them, and re-layouts  1.67 us

profile of v7, /device:TPU:1, one launch (start us, length us, event | category | flops | bytes accessed | tf_op | source)
XLA Modules:
  0.0 44.4 jit_solution(6427384527280375691)
XLA Ops:
  0.0 42.7 %panel.1 = f32[1,2,32,1024]{3,2,1,0:T(8,128)} custom-call(f32[2,8,256]{2,1,0:T(8,128)} %bitcast.9, f32[64,128]{1,0:T(8,128)} %pot_in.1, f32[2048,128]{1,0:T(8,128)} %bitcast.7, s32[128,128]{1,0:T(8,128)} %bitcast.8, s32[32]{0:T(128)} %counts_in.1, bf16[256,512]{1,0:T(8,128)(2,1)} %constant.16.clone.wz_h_in, bf16[256,512]{1,0:T(8,128)(2,1)} %constant.17.clone.wz_l_in, ...), custom_call_target="tpu_custom_call" | custom-call | tf_op jit(solution)/shard_map/panel/pallas_call | solution.py:466
  42.7 1.7 %copy.16 = f32[1,2,32,1024]{3,2,1,0:T(8,128)} copy(f32[1,2,32,1024]{3,2,1,0:T(8,128)} %panel.1) | data formatting | bytes 524288
